TPU v7x, 128 devices: a whole 4x4x4 slice. The times are simulated.
128 devices in a mesh: tm: 64 (over y, z, x_lo, core), asset: 2 (over x_hi).
Axes of the slice: x: 4 (x_hi: 2, x_lo: 2; x = x_hi * 2 + x_lo), y: 4, z: 4, core: 2. Of those that a mesh axis runs over, the one named last changes fastest.
Arguments:
- tick_bars: float32 [2, 64, 61440], P('asset', 'tm'), may hold values from -20 to 20
- prior_bars: float32 [2, 64, 1600], P('asset', 'tm'), may hold values from -20 to 20, as said below
Outputs:
- connectedness: float32 [192, 8192], P('tm', 'asset')
Inputs may be any that keep to these rules, and one draw needn't show every extreme that they name: `prior_bars`: bar returns of the same assets.
All inputs are finite; a program needn't handle non-finite values.
Results may differ from a plain program's by a relative error of at most 0.0014.
Values may be sent and summed in bfloat16 or wider, within the bound.
A program may use at most 64 MiB of HBM per device.

v0:
```python
import math

import jax
import jax.numpy as jnp
from jax import lax
from jax.sharding import PartitionSpec as P

ASSETS = 8192
SPAN = 30
STRIDE = 5
WIN_DEV = 3
LEAD = 25


FLOOR_SQUARES = 1.0


def from_behind(x, axis, by):
    size = lax.axis_size(axis)
    pairs = [(i, i + by) for i in range(size) if 0 <= i + by < size]
    return lax.ppermute(x, axis, pairs)


def from_everyone(x, axis):
    size = lax.axis_size(axis)
    return lax.all_to_all(jnp.broadcast_to(x[None], (size, *x.shape)), axis, 0, 0, tiled=True)


def laid_out(pieces, dim):
    shape = list(pieces.shape[1:])
    shape[dim] *= pieces.shape[0]
    return jnp.moveaxis(pieces, 0, dim).reshape(shape)


def collect(x, axis, dim):
    pieces = from_everyone(x, axis)
    return laid_out(pieces, dim)


def swapped(block, axis, distance):
    count = lax.axis_size(axis)
    route = []
    for low in range(count):
        high = low | 1 << distance
        if high != low and high < count:
            route += [(low, high), (high, low)]
    return lax.ppermute(block, axis, route)


def window_stack(extended):
    columns = extended.shape[1]
    groups = extended.reshape(-1, STRIDE, columns)
    stacked = jnp.stack(
        [groups[offset : offset + WIN_DEV] for offset in range(SPAN // STRIDE)], axis=1
    )
    values = stacked.reshape(WIN_DEV, SPAN, columns)
    centred = values - jnp.mean(values, axis=1, keepdims=True)
    squares = jnp.sum(centred * centred, axis=1, keepdims=True)
    return (centred * lax.rsqrt(jnp.maximum(squares, FLOOR_SQUARES))).astype(jnp.bfloat16)


def block_magnitude(left_part, right_part, offset, block_rows):
    correlation = lax.dot_general(
        left_part[:, offset : offset + block_rows],
        right_part,
        (((0,), (0,)), ((), ())),
        preferred_element_type=jnp.float32,
    )
    return jnp.abs(correlation.astype(jnp.bfloat16)).astype(jnp.float32)


def row_totals(own_windows, other_windows):
    columns = own_windows.shape[2]
    block_rows = min(1024, columns)

    def row_one_window(operands):
        left_part, right_part = operands
        pieces = [
            jnp.sum(block_magnitude(left_part, right_part, offset, block_rows), axis=1)
            for offset in range(0, columns, block_rows)
        ]
        return jnp.concatenate(pieces)

    return lax.map(row_one_window, (own_windows, other_windows))


def both_totals(own_windows, other_windows):
    columns = own_windows.shape[2]
    block_rows = min(1024, columns)

    def both_one_window(operands):
        left_part, right_part = operands
        pieces = []
        column_total = jnp.zeros((right_part.shape[1],), jnp.float32)
        for offset in range(0, columns, block_rows):
            magnitude = block_magnitude(left_part, right_part, offset, block_rows)
            pieces.append(jnp.sum(magnitude, axis=1))
            column_total = column_total + jnp.sum(magnitude, axis=0)
        return (jnp.concatenate(pieces), column_total)

    return lax.map(both_one_window, (own_windows, other_windows))


def earlier_rows(tail_rows, distance):
    return from_behind(tail_rows, "tm", distance)


def time_block_rows(tick_bars, prior_bars):
    groups = lax.axis_size("tm")
    group_cols = ASSETS // (2 * groups)
    outgoing = tick_bars.reshape(groups, 1, -1)
    arrived = lax.all_to_all(outgoing, "tm", split_axis=0, concat_axis=1, tiled=True)
    block_len = arrived.shape[2] // group_cols
    own_rows = jnp.transpose(arrived.reshape(groups, block_len, group_cols), (1, 0, 2)).reshape(
        block_len, groups * group_cols
    )
    prior_all = collect(prior_bars, "tm", 1)
    series_prior = jnp.transpose(prior_all.reshape(groups, LEAD, group_cols), (1, 0, 2)).reshape(
        LEAD, groups * group_cols
    )
    reach = (LEAD + block_len - 1) // block_len
    earlier = []
    for distance in range(reach, 0, -1):
        needed = min(block_len, LEAD - (distance - 1) * block_len)
        earlier.append(earlier_rows(own_rows[block_len - needed :], distance))
    history = jnp.concatenate(earlier, axis=0)
    position = lax.axis_index("tm")
    first_row = position * block_len
    padded = jnp.concatenate([series_prior, jnp.zeros_like(series_prior)], axis=0)
    from_prior = lax.dynamic_slice_in_dim(padded, jnp.minimum(first_row, LEAD), LEAD, 0)
    before_start = first_row - LEAD + jnp.arange(LEAD, dtype=jnp.int32) < 0
    history = jnp.where(before_start[:, None], from_prior, history)
    return jnp.concatenate([history, own_rows], axis=0)


def shards(tick_bars, prior_bars):
    extended = time_block_rows(tick_bars, prior_bars)
    scaled = window_stack(extended)
    columns = scaled.shape[2]
    empty = jnp.zeros((WIN_DEV, columns), jnp.float32)
    partner = swapped(scaled, "asset", 0)
    tile_index = lax.axis_index("asset")
    quarter = columns // 2
    diagonal_part = row_totals(scaled, scaled)
    column_part = empty
    cross_rows = []
    for half_index in range(2):
        mine = scaled[:, :, half_index * quarter : (half_index + 1) * quarter]
        target = (half_index + tile_index) % 2
        theirs = lax.dynamic_slice_in_dim(partner, target * quarter, quarter, 2)
        row_add, column_add = both_totals(mine, theirs)
        cross_rows.append(row_add)
        column_part = lax.dynamic_update_slice_in_dim(column_part, column_add, target * quarter, 1)
    returned = swapped(column_part.astype(jnp.bfloat16), "asset", 0).astype(column_part.dtype)
    totals = diagonal_part + jnp.concatenate(cross_rows, axis=1) + returned
    return totals * (math.sqrt(SPAN) / ASSETS)


def solution(mesh):
    in_specs = (P("asset", "tm", None), P("asset", "tm", None))
    out_specs = P("tm", "asset")
    return jax.shard_map(shards, mesh=mesh, in_specs=in_specs, out_specs=out_specs, check_vma=False)
```

profile of v0, /device:TPU:8, one launch (start us, length us, event | category | flops | bytes accessed | tf_op | source)
XLA Modules:
  0.0 133.8 jit_solution(8419375596661278419)
XLA Ops:
  0.5 2.2 %reduce.14 = f32[61440]{0:T(1024)S(1)} reduce(f32[1,1,61440]{2,1,0:T(1,128)} %param.8, f32[]{:T(128)} %broadcast.44), dimensions={0,1}, to_apply=%param.8.reduce_sub_computation.3 | reduce | bytes 491524 | tf_op args[0]
  2.7 1.0 reshape.82
  3.7 9.9 %all-to-all-start.1 = ((f32[64,1,960]{2,1,0:T(1,128)}), f32[64,1,960]{2,1,0:T(1,128)S(1)}, u32[]{:S(2)}, u32[]{:S(2)}) async-start(f32[64,1,960]{2,1,0:T(1,128)} %reshape.82), calls=%async_computation.1 | async-start | bytes 524288 | tf_op jit(solution)/shard_map/all_to_all | solution.py:112
  14.3 8.1 %all-to-all-done.1 = f32[64,1,960]{2,1,0:T(1,128)S(1)} async-done(((f32[64,1,960]{2,1,0:T(1,128)}), f32[64,1,960]{2,1,0:T(1,128)S(1)}, u32[]{:S(2)}, u32[]{:S(2)}) %all-to-all-start.1) | async-done | bytes 245792 | tf_op jit(solution)/shard_map/all_to_all | solution.py:112
  22.4 1.0 broadcast_in_dim.35
  23.4 5.7 %all-to-all-start = ((f32[64,1,1,1600]{3,2,1,0:T(1,128)}), f32[64,1,1,1600]{3,2,1,0:T(1,128)S(1)}, u32[]{:S(2)}, u32[]{:S(2)}) async-start(f32[64,1,1,1600]{3,2,1,0:T(1,128)} %broadcast_in_dim.35), calls=%async_computation | async-start | bytes 851968 | tf_op jit(solution)/shard_map/all_to_all | solution.py:26
  30.3 2.0 %collective-permute-start.1 = (f32[15,4096]{1,0:T(8,128)S(1)}, f32[15,4096]{1,0:T(8,128)S(1)}, u32[]{:S(2)}, u32[]{:S(2)}) collective-permute-start(f32[15,4096]{1,0:T(8,128)S(1)} %reshape.84), channel_id=1, source_target_pairs={{0,2},{2,4},{4,6},{6,8},{8,10},{10,12},{12,14},{14,16},{16,18},{18... | collective-permute-start | bytes 737288 | tf_op jit(solution)/shard_map/ppermute | solution.py:21
  32.6 3.4 %collective-permute-start = (f32[10,4096]{1,0:T(8,128)S(1)}, f32[10,4096]{1,0:T(8,128)S(1)}, u32[]{:S(2)}, u32[]{:S(2)}) collective-permute-start(f32[10,4096]{1,0:T(8,128)S(1)} %slice.62), channel_id=1, source_target_pairs={{0,4},{2,6},{4,8},{6,10},{8,12},{10,14},{12,16},{14,18},{16,20},{1... | collective-permute-start | bytes 491528 | tf_op jit(solution)/shard_map/ppermute | solution.py:21
  36.2 3.8 %all-to-all-done = f32[64,1,1,1600]{3,2,1,0:T(1,128)S(1)} async-done(((f32[64,1,1,1600]{3,2,1,0:T(1,128)}), f32[64,1,1,1600]{3,2,1,0:T(1,128)S(1)}, u32[]{:S(2)}, u32[]{:S(2)}) %all-to-all-start) | async-done | bytes 409632 | tf_op jit(solution)/shard_map/all_to_all | solution.py:26
  40.0 1.0 reduce.9
  42.1 4.5 %collective-permute-done = f32[10,4096]{1,0:T(8,128)S(1)} collective-permute-done((f32[10,4096]{1,0:T(8,128)S(1)}, f32[10,4096]{1,0:T(8,128)S(1)}, u32[]{:S(2)}, u32[]{:S(2)}) %collective-permute-start) | collective-permute-done | bytes 163872 | tf_op jit(solution)/shard_map/ppermute | solution.py:21
  48.5 1.7 %stack.22 = f32[3,1,5,4096]{3,2,0,1:T(8,128)} reshape(f32[15,4096]{1,0:T(8,128)} %get-tuple-element.124) | data formatting | bytes 491520 | tf_op jit(solution)/shard_map/stack | solution.py:53
  51.0 1.0 stack.24
  52.0 1.0 stack.25
  53.0 1.1 fusion.24
  54.2 1.1 fusion.26
  55.8 1.6 %copy.15 = f32[3,6,5,4096]{3,2,1,0:T(8,128)} copy(f32[3,6,5,4096]{3,2,0,1:T(8,128)S(1)} %get-tuple-element.137) | data formatting | bytes 2949120 | tf_op jit(solution)/shard_map/stack | solution.py:53
  57.9 1.7 %reshape.85 = f32[3,30,4096]{2,1,0:T(8,128)S(1)} reshape(f32[3,6,5,4096]{3,2,1,0:T(8,128)} %copy.15) | data formatting | bytes 2949120 | tf_op jit(solution)/shard_map/reshape | solution.py:56
  59.8 3.0 %collective-permute-start.2 = (bf16[3,30,4096]{2,1,0:T(8,128)(2,1)S(1)}, bf16[3,30,4096]{2,1,0:T(8,128)(2,1)S(1)}, u32[]{:S(2)}, u32[]{:S(2)}) collective-permute-start(bf16[3,30,4096]{2,1,0:T(8,128)(2,1)S(1)} %multiply_convert_fusion), channel_id=1, source_target_pairs={{0,1},{1,0},{2,3},{3,2},{4,5},{5,4},{6,7},{7,6},{8,9},{9,8},{10,11... | collective-permute-start | bytes 2211848 | tf_op jit(solution)/shard_map/ppermute | solution.py:47
  62.8 18.4 %collective-permute-done.2 = bf16[3,30,4096]{2,1,0:T(8,128)(2,1)S(1)} collective-permute-done((bf16[3,30,4096]{2,1,0:T(8,128)(2,1)S(1)}, bf16[3,30,4096]{2,1,0:T(8,128)(2,1)S(1)}, u32[]{:S(2)}, u32[]{:S(2)}) %collective-permute-start.2) | collective-permute-done | bytes 737312 | tf_op jit(solution)/shard_map/ppermute | solution.py:47
  81.3 9.2 %while.35 = (s32[]{:T(128)}, f32[3,2048]{1,0:T(4,128)S(1)}, f32[3,2048]{1,0:T(4,128)S(1)}, bf16[3,30,2048]{2,1,0:T(8,128)(2,1)S(1)}, bf16[3,30,2048]{2,1,0:T(8,128)(2,1)S(1)}, /*index=5*/s32[]{:T(128)}, s32[]{:T(128)}) while((s32[]{:T(128)}, f32[3,2048]{1,0:T(4,128)S(1)}, f32[3,2048]{1,0:T(4,128)S(1)}, bf16[3,30,2048]{2,1,0:T(8,128)(2,1)S(1)}, ...), condition=%wide.region_18.19_spmd, body=%wide.region_13.18_spmd.sunk | while | flops 272627712 | bytes 737377 | solution.py:101
  81.4 1.4 %convert_reduce_fusion.25 = (f32[2048]{0:T(1024)S(1)}, f32[1024]{0:T(1024)S(1)}) fusion(bf16[3,30,2048]{2,1,0:T(8,128)(2,1)S(1)} %get-tuple-element.289, s32[]{:T(128)} %get-tuple-element.278, bf16[30,2048]{1,0:T(8,128)(2,1)S(1)} %dynamic-slice_bitcast_fusion.7), kind=kOutput, calls=%fused_computation.12.clone.1 | convolution fusion | flops 136311808 | bytes 208900 | tf_op jit(solution)/shard_map/while/body/eval_jaxpr/dot_general | solution.py:63
  82.7 1.4 %convert_reduce_fusion.24 = (f32[2048]{0:T(1024)S(1)}, f32[1024]{0:T(1024)S(1)}) fusion(bf16[3,30,2048]{2,1,0:T(8,128)(2,1)S(1)} %get-tuple-element.289, s32[]{:T(128)} %get-tuple-element.278, bf16[30,2048]{1,0:T(8,128)(2,1)S(1)} %dynamic-slice_bitcast_fusion.7), kind=kOutput, calls=%fused_computation.10.clone.1 | convolution fusion | flops 136311808 | bytes 208900 | tf_op jit(solution)/shard_map/while/body/eval_jaxpr/dot_general | solution.py:63
  84.4 1.4 %convert_reduce_fusion.25 = (f32[2048]{0:T(1024)S(1)}, f32[1024]{0:T(1024)S(1)}) fusion(bf16[3,30,2048]{2,1,0:T(8,128)(2,1)S(1)} %get-tuple-element.289, s32[]{:T(128)} %get-tuple-element.278, bf16[30,2048]{1,0:T(8,128)(2,1)S(1)} %dynamic-slice_bitcast_fusion.7), kind=kOutput, calls=%fused_computation.12.clone.1 | convolution fusion | flops 136311808 | bytes 208900 | tf_op jit(solution)/shard_map/while/body/eval_jaxpr/dot_general | solution.py:63
  85.8 1.4 %convert_reduce_fusion.24 = (f32[2048]{0:T(1024)S(1)}, f32[1024]{0:T(1024)S(1)}) fusion(bf16[3,30,2048]{2,1,0:T(8,128)(2,1)S(1)} %get-tuple-element.289, s32[]{:T(128)} %get-tuple-element.278, bf16[30,2048]{1,0:T(8,128)(2,1)S(1)} %dynamic-slice_bitcast_fusion.7), kind=kOutput, calls=%fused_computation.10.clone.1 | convolution fusion | flops 136311808 | bytes 208900 | tf_op jit(solution)/shard_map/while/body/eval_jaxpr/dot_general | solution.py:63
  87.5 1.4 %convert_reduce_fusion.25 = (f32[2048]{0:T(1024)S(1)}, f32[1024]{0:T(1024)S(1)}) fusion(bf16[3,30,2048]{2,1,0:T(8,128)(2,1)S(1)} %get-tuple-element.289, s32[]{:T(128)} %get-tuple-element.278, bf16[30,2048]{1,0:T(8,128)(2,1)S(1)} %dynamic-slice_bitcast_fusion.7), kind=kOutput, calls=%fused_computation.12.clone.1 | convolution fusion | flops 136311808 | bytes 208900 | tf_op jit(solution)/shard_map/while/body/eval_jaxpr/dot_general | solution.py:63
  88.8 1.4 %convert_reduce_fusion.24 = (f32[2048]{0:T(1024)S(1)}, f32[1024]{0:T(1024)S(1)}) fusion(bf16[3,30,2048]{2,1,0:T(8,128)(2,1)S(1)} %get-tuple-element.289, s32[]{:T(128)} %get-tuple-element.278, bf16[30,2048]{1,0:T(8,128)(2,1)S(1)} %dynamic-slice_bitcast_fusion.7), kind=kOutput, calls=%fused_computation.10.clone.1 | convolution fusion | flops 136311808 | bytes 208900 | tf_op jit(solution)/shard_map/while/body/eval_jaxpr/dot_general | solution.py:63
  90.5 9.2 %while.36 = (s32[]{:T(128)}, f32[3,2048]{1,0:T(4,128)S(1)}, f32[3,2048]{1,0:T(4,128)S(1)}, bf16[3,30,2048]{2,1,0:T(8,128)(2,1)S(1)}, bf16[3,30,2048]{2,1,0:T(8,128)(2,1)S(1)}, /*index=5*/s32[]{:T(128)}, s32[]{:T(128)}) while((s32[]{:T(128)}, f32[3,2048]{1,0:T(4,128)S(1)}, f32[3,2048]{1,0:T(4,128)S(1)}, bf16[3,30,2048]{2,1,0:T(8,128)(2,1)S(1)}, ...), condition=%wide.region_24.25_spmd, body=%wide.region_19.24_spmd.sunk | while | flops 272627712 | bytes 737377 | solution.py:101
  90.6 1.4 %convert_reduce_fusion.27 = (f32[2048]{0:T(1024)S(1)}, f32[1024]{0:T(1024)S(1)}) fusion(bf16[3,30,2048]{2,1,0:T(8,128)(2,1)S(1)} %get-tuple-element.268, s32[]{:T(128)} %get-tuple-element.257, bf16[30,2048]{1,0:T(8,128)(2,1)S(1)} %dynamic-slice_bitcast_fusion.8), kind=kOutput, calls=%fused_computation.28.clone.1 | convolution fusion | flops 136311808 | bytes 208900 | tf_op jit(solution)/shard_map/while/body/eval_jaxpr/dot_general | solution.py:63
  91.9 1.4 %convert_reduce_fusion.26 = (f32[2048]{0:T(1024)S(1)}, f32[1024]{0:T(1024)S(1)}) fusion(bf16[3,30,2048]{2,1,0:T(8,128)(2,1)S(1)} %get-tuple-element.268, s32[]{:T(128)} %get-tuple-element.257, bf16[30,2048]{1,0:T(8,128)(2,1)S(1)} %dynamic-slice_bitcast_fusion.8), kind=kOutput, calls=%fused_computation.26.clone.1 | convolution fusion | flops 136311808 | bytes 208900 | tf_op jit(solution)/shard_map/while/body/eval_jaxpr/dot_general | solution.py:63
  93.6 1.4 %convert_reduce_fusion.27 = (f32[2048]{0:T(1024)S(1)}, f32[1024]{0:T(1024)S(1)}) fusion(bf16[3,30,2048]{2,1,0:T(8,128)(2,1)S(1)} %get-tuple-element.268, s32[]{:T(128)} %get-tuple-element.257, bf16[30,2048]{1,0:T(8,128)(2,1)S(1)} %dynamic-slice_bitcast_fusion.8), kind=kOutput, calls=%fused_computation.28.clone.1 | convolution fusion | flops 136311808 | bytes 208900 | tf_op jit(solution)/shard_map/while/body/eval_jaxpr/dot_general | solution.py:63
  95.0 1.4 %convert_reduce_fusion.26 = (f32[2048]{0:T(1024)S(1)}, f32[1024]{0:T(1024)S(1)}) fusion(bf16[3,30,2048]{2,1,0:T(8,128)(2,1)S(1)} %get-tuple-element.268, s32[]{:T(128)} %get-tuple-element.257, bf16[30,2048]{1,0:T(8,128)(2,1)S(1)} %dynamic-slice_bitcast_fusion.8), kind=kOutput, calls=%fused_computation.26.clone.1 | convolution fusion | flops 136311808 | bytes 208900 | tf_op jit(solution)/shard_map/while/body/eval_jaxpr/dot_general | solution.py:63
  96.7 1.4 %convert_reduce_fusion.27 = (f32[2048]{0:T(1024)S(1)}, f32[1024]{0:T(1024)S(1)}) fusion(bf16[3,30,2048]{2,1,0:T(8,128)(2,1)S(1)} %get-tuple-element.268, s32[]{:T(128)} %get-tuple-element.257, bf16[30,2048]{1,0:T(8,128)(2,1)S(1)} %dynamic-slice_bitcast_fusion.8), kind=kOutput, calls=%fused_computation.28.clone.1 | convolution fusion | flops 136311808 | bytes 208900 | tf_op jit(solution)/shard_map/while/body/eval_jaxpr/dot_general | solution.py:63
  98.0 1.4 %convert_reduce_fusion.26 = (f32[2048]{0:T(1024)S(1)}, f32[1024]{0:T(1024)S(1)}) fusion(bf16[3,30,2048]{2,1,0:T(8,128)(2,1)S(1)} %get-tuple-element.268, s32[]{:T(128)} %get-tuple-element.257, bf16[30,2048]{1,0:T(8,128)(2,1)S(1)} %dynamic-slice_bitcast_fusion.8), kind=kOutput, calls=%fused_computation.26.clone.1 | convolution fusion | flops 136311808 | bytes 208900 | tf_op jit(solution)/shard_map/while/body/eval_jaxpr/dot_general | solution.py:63
  99.8 3.0 %collective-permute-start.3 = (bf16[3,4096]{1,0:T(4,128)(2,1)S(1)}, bf16[3,4096]{1,0:T(4,128)(2,1)S(1)}, u32[]{:S(2)}, u32[]{:S(2)}) collective-permute-start(bf16[3,4096]{1,0:T(4,128)(2,1)S(1)} %convert_element_type.58), channel_id=1, source_target_pairs={{0,1},{1,0},{2,3},{3,2},{4,5},{5,4},{6,7},{7,6},{8,9},{9,8},{10,11... | collective-permute-start | bytes 73736 | tf_op jit(solution)/shard_map/ppermute | solution.py:47
  102.8 30.3 %while.34 = (s32[]{:T(128)}, f32[3,4096]{1,0:T(4,128)S(1)}, bf16[3,30,4096]{2,1,0:T(8,128)(2,1)S(1)}, s32[]{:T(128)}, s32[]{:T(128)}) while((s32[]{:T(128)}, f32[3,4096]{1,0:T(4,128)S(1)}, bf16[3,30,4096]{2,1,0:T(8,128)(2,1)S(1)}, s32[]{:T(128)}, s32[]{:T(128)}) %tuple.68), condition=%wide.region_12.13_spmd, body=%wide.region_7.12_spmd.sunk | while | flops 1073750016 | bytes 1884229 | solution.py:84
  102.9 2.4 %convert_reduce_fusion.20 = f32[1024]{0:T(1024)S(1)} fusion(bf16[30,4096]{1,0:T(8,128)(2,1)S(1)} %dynamic-slice_bitcast_fusion.6), kind=kOutput, calls=%fused_computation.clone.1 | convolution fusion | flops 268434432 | bytes 331776 | tf_op jit(solution)/shard_map/while/body/eval_jaxpr/dot_general | solution.py:63
  105.3 2.5 %convert_reduce_fusion.21 = f32[1024]{0:T(1024)S(1)} fusion(bf16[30,4096]{1,0:T(8,128)(2,1)S(1)} %dynamic-slice_bitcast_fusion.6), kind=kOutput, calls=%fused_computation.1.clone.1 | convolution fusion | flops 268434432 | bytes 331776 | tf_op jit(solution)/shard_map/while/body/eval_jaxpr/dot_general | solution.py:63
  107.8 2.5 %convert_reduce_fusion.22 = f32[1024]{0:T(1024)S(1)} fusion(bf16[30,4096]{1,0:T(8,128)(2,1)S(1)} %dynamic-slice_bitcast_fusion.6), kind=kOutput, calls=%fused_computation.2.clone.1 | convolution fusion | flops 268434432 | bytes 331776 | tf_op jit(solution)/shard_map/while/body/eval_jaxpr/dot_general | solution.py:63
  110.2 2.5 %convert_reduce_fusion.23 = f32[1024]{0:T(1024)S(1)} fusion(bf16[30,4096]{1,0:T(8,128)(2,1)S(1)} %dynamic-slice_bitcast_fusion.6), kind=kOutput, calls=%fused_computation.3.clone.1 | convolution fusion | flops 268434432 | bytes 331776 | tf_op jit(solution)/shard_map/while/body/eval_jaxpr/dot_general | solution.py:63
  113.0 2.4 %convert_reduce_fusion.20 = f32[1024]{0:T(1024)S(1)} fusion(bf16[30,4096]{1,0:T(8,128)(2,1)S(1)} %dynamic-slice_bitcast_fusion.6), kind=kOutput, calls=%fused_computation.clone.1 | convolution fusion | flops 268434432 | bytes 331776 | tf_op jit(solution)/shard_map/while/body/eval_jaxpr/dot_general | solution.py:63
  115.4 2.5 %convert_reduce_fusion.21 = f32[1024]{0:T(1024)S(1)} fusion(bf16[30,4096]{1,0:T(8,128)(2,1)S(1)} %dynamic-slice_bitcast_fusion.6), kind=kOutput, calls=%fused_computation.1.clone.1 | convolution fusion | flops 268434432 | bytes 331776 | tf_op jit(solution)/shard_map/while/body/eval_jaxpr/dot_general | solution.py:63
  117.9 2.5 %convert_reduce_fusion.22 = f32[1024]{0:T(1024)S(1)} fusion(bf16[30,4096]{1,0:T(8,128)(2,1)S(1)} %dynamic-slice_bitcast_fusion.6), kind=kOutput, calls=%fused_computation.2.clone.1 | convolution fusion | flops 268434432 | bytes 331776 | tf_op jit(solution)/shard_map/while/body/eval_jaxpr/dot_general | solution.py:63
  120.3 2.5 %convert_reduce_fusion.23 = f32[1024]{0:T(1024)S(1)} fusion(bf16[30,4096]{1,0:T(8,128)(2,1)S(1)} %dynamic-slice_bitcast_fusion.6), kind=kOutput, calls=%fused_computation.3.clone.1 | convolution fusion | flops 268434432 | bytes 331776 | tf_op jit(solution)/shard_map/while/body/eval_jaxpr/dot_general | solution.py:63
  123.1 2.4 %convert_reduce_fusion.20 = f32[1024]{0:T(1024)S(1)} fusion(bf16[30,4096]{1,0:T(8,128)(2,1)S(1)} %dynamic-slice_bitcast_fusion.6), kind=kOutput, calls=%fused_computation.clone.1 | convolution fusion | flops 268434432 | bytes 331776 | tf_op jit(solution)/shard_map/while/body/eval_jaxpr/dot_general | solution.py:63
  125.5 2.5 %convert_reduce_fusion.21 = f32[1024]{0:T(1024)S(1)} fusion(bf16[30,4096]{1,0:T(8,128)(2,1)S(1)} %dynamic-slice_bitcast_fusion.6), kind=kOutput, calls=%fused_computation.1.clone.1 | convolution fusion | flops 268434432 | bytes 331776 | tf_op jit(solution)/shard_map/while/body/eval_jaxpr/dot_general | solution.py:63
  128.0 2.5 %convert_reduce_fusion.22 = f32[1024]{0:T(1024)S(1)} fusion(bf16[30,4096]{1,0:T(8,128)(2,1)S(1)} %dynamic-slice_bitcast_fusion.6), kind=kOutput, calls=%fused_computation.2.clone.1 | convolution fusion | flops 268434432 | bytes 331776 | tf_op jit(solution)/shard_map/while/body/eval_jaxpr/dot_general | solution.py:63
  130.4 2.5 %convert_reduce_fusion.23 = f32[1024]{0:T(1024)S(1)} fusion(bf16[30,4096]{1,0:T(8,128)(2,1)S(1)} %dynamic-slice_bitcast_fusion.6), kind=kOutput, calls=%fused_computation.3.clone.1 | convolution fusion | flops 268434432 | bytes 331776 | tf_op jit(solution)/shard_map/while/body/eval_jaxpr/dot_general | solution.py:63
  (81 shorter events, 11.1 us)
Async XLA Ops:
  3.7 18.8 %all-to-all-start.1 = ((f32[64,1,960]{2,1,0:T(1,128)}), f32[64,1,960]{2,1,0:T(1,128)S(1)}, u32[]{:S(2)}, u32[]{:S(2)}) async-start(f32[64,1,960]{2,1,0:T(1,128)} %reshape.82), calls=%async_computation.1 | async-start | bytes 524288 | tf_op jit(solution)/shard_map/all_to_all | solution.py:112
  23.4 16.6 %all-to-all-start = ((f32[64,1,1,1600]{3,2,1,0:T(1,128)}), f32[64,1,1,1600]{3,2,1,0:T(1,128)S(1)}, u32[]{:S(2)}, u32[]{:S(2)}) async-start(f32[64,1,1,1600]{3,2,1,0:T(1,128)} %broadcast_in_dim.35), calls=%async_computation | async-start | bytes 851968 | tf_op jit(solution)/shard_map/all_to_all | solution.py:26
  30.3 16.3 %collective-permute-start.1 = (f32[15,4096]{1,0:T(8,128)S(1)}, f32[15,4096]{1,0:T(8,128)S(1)}, u32[]{:S(2)}, u32[]{:S(2)}) collective-permute-start(f32[15,4096]{1,0:T(8,128)S(1)} %reshape.84), channel_id=1, source_target_pairs={{0,2},{2,4},{4,6},{6,8},{8,10},{10,12},{12,14},{14,16},{16,18},{18... | collective-permute-start | bytes 737288 | tf_op jit(solution)/shard_map/ppermute | solution.py:21
  32.6 14.0 %collective-permute-start = (f32[10,4096]{1,0:T(8,128)S(1)}, f32[10,4096]{1,0:T(8,128)S(1)}, u32[]{:S(2)}, u32[]{:S(2)}) collective-permute-start(f32[10,4096]{1,0:T(8,128)S(1)} %slice.62), channel_id=1, source_target_pairs={{0,4},{2,6},{4,8},{6,10},{8,12},{10,14},{12,16},{14,18},{16,20},{1... | collective-permute-start | bytes 491528 | tf_op jit(solution)/shard_map/ppermute | solution.py:21
  55.8 1.6 %copy-start = (f32[3,4096]{1,0:T(4,128)S(1)}, f32[3,4096]{1,0:T(4,128)}, u32[]{:S(2)}) copy-start(f32[3,4096]{1,0:T(4,128)} %get-tuple-element.128) | copy-start | bytes 147460
  59.8 21.5 %collective-permute-start.2 = (bf16[3,30,4096]{2,1,0:T(8,128)(2,1)S(1)}, bf16[3,30,4096]{2,1,0:T(8,128)(2,1)S(1)}, u32[]{:S(2)}, u32[]{:S(2)}) collective-permute-start(bf16[3,30,4096]{2,1,0:T(8,128)(2,1)S(1)} %multiply_convert_fusion), channel_id=1, source_target_pairs={{0,1},{1,0},{2,3},{3,2},{4,5},{5,4},{6,7},{7,6},{8,9},{9,8},{10,11... | collective-permute-start | bytes 2211848 | tf_op jit(solution)/shard_map/ppermute | solution.py:47
  99.8 33.4 %collective-permute-start.3 = (bf16[3,4096]{1,0:T(4,128)(2,1)S(1)}, bf16[3,4096]{1,0:T(4,128)(2,1)S(1)}, u32[]{:S(2)}, u32[]{:S(2)}) collective-permute-start(bf16[3,4096]{1,0:T(4,128)(2,1)S(1)} %convert_element_type.58), channel_id=1, source_target_pairs={{0,1},{1,0},{2,3},{3,2},{4,5},{5,4},{6,7},{7,6},{8,9},{9,8},{10,11... | collective-permute-start | bytes 73736 | tf_op jit(solution)/shard_map/ppermute | solution.py:47
where the time goes:
time: 134 us
  matrix products  45.7 us (34%)
  waiting for transfers between devices  34.8 us (26%)
  starting transfers between devices  27 us (20%)
  local copies, waits for them, and re-layouts  15 us (11%)
  other arithmetic  10.6 us (8%)
    dot_general x24, matrix products, block_magnitude(): lax.dot_general(left_part[:, offset:offset + block_rows], right_part, (((...  45.7 us
    ppermute x2, waiting for transfers between devices, swapped(): return lax.ppermute(block, axis, route)  18.4 us
    all_to_all x1, starting transfers between devices, time_block_rows(): lax.all_to_all(outgoing, 'tm', split_axis=0, concat_axis=1, tiled=True)  9.88 us
    all_to_all x1, waiting for transfers between devices, time_block_rows(): lax.all_to_all(outgoing, 'tm', split_axis=0, concat_axis=1, tiled=True)  8.14 us
    another operation x7, local copies, waits for them, and re-layouts, window_stack(): jnp.stack([groups[offset:offset + WIN_DEV] for offset in range(SPAN // ST...  6.24 us
    ppermute x2, starting transfers between devices, swapped(): return lax.ppermute(block, axis, route)  6.01 us
    all_to_all x1, starting transfers between devices, from_everyone(): lax.all_to_all(jnp.broadcast_to(x[None], (size, *x.shape)), axis, 0, 0, t...  5.72 us
    ppermute x2, starting transfers between devices, from_behind(): return lax.ppermute(x, axis, pairs)  5.42 us
  transfers between devices with their start and end apart: 6, of which 4 were waited for; matrix products, arithmetic and copies ran while one was open for 26% of the time, Pallas kernels for 0%

commit v1 on v0

v1 whole, which is shorter than its diff:
```python
import functools
import math

import jax
import jax.numpy as jnp
from jax import lax
from jax.experimental import pallas as pl
from jax.experimental.pallas import tpu as pltpu
from jax.sharding import PartitionSpec as P

ASSETS = 8192
SPAN = 30
STRIDE = 5
WIN_DEV = 3
LEAD = 25
FLOOR_SQUARES = 1.0

MESH = pl.DeviceIdType.MESH
TILE = ASSETS // 2
GROUPS = 64
GROUP_COLS = TILE // GROUPS
BLOCK_BARS = WIN_DEV * STRIDE
LEAD_ROWS = 13
TICK_ROWS = 480
PAD_ROWS = 16
SERIES_ROWS = LEAD_ROWS + TICK_ROWS + PAD_ROWS - LEAD_ROWS
MSG_ROWS = 21
SLOT_ROWS = 24
BLOCK = 256
HALF = TILE // 2
EXT = TILE + HALF
UNROLL = 2


def place():
    tm = lax.axis_index("tm")
    return tm // 2, lax.rem(tm, 2), lax.axis_index("asset")


def gather_kernel(tick_ref, prior_ref, own_ref, other_ref, series, load_sem, send_sem, pass_sem, own_sem, other_sem):
    pair, core, half = place()
    me = pair * 2 + core
    loads = [
        pltpu.make_async_copy(prior_ref.at[pl.ds(0, LEAD_ROWS)], series.at[pl.ds(0, LEAD_ROWS)], load_sem.at[0]),
        pltpu.make_async_copy(tick_ref, series.at[pl.ds(LEAD_ROWS, TICK_ROWS)], load_sem.at[1]),
        pltpu.make_async_copy(
            prior_ref.at[pl.ds(LEAD_ROWS, PAD_ROWS - LEAD_ROWS)],
            series.at[pl.ds(LEAD_ROWS + TICK_ROWS, PAD_ROWS - LEAD_ROWS)],
            load_sem.at[2],
        ),
    ]
    for load in loads:
        load.start()

    barrier = pltpu.get_barrier_semaphore()

    def greet(g, carry):
        @pl.when(jnp.logical_or(g != me, core != half))
        def _():
            pl.semaphore_signal(barrier, inc=1, device_id=(g, core), device_id_type=MESH)

        return carry

    lax.fori_loop(0, GROUPS, greet, 0)
    pl.semaphore_signal(barrier, inc=1, device_id=(pair * 2 + 1 - core, half), device_id_type=MESH)
    pl.semaphore_wait(barrier, GROUPS + jnp.where(core == half, 0, 1))
    for load in loads:
        load.wait()

    def message(k):
        target_pair = lax.bitwise_xor(pair, k // 2)
        target_half = lax.bitwise_xor(half, lax.rem(k, 2))
        start = (BLOCK_BARS * (2 * target_pair + target_half) + 1) // 2
        return target_pair, target_half, series.at[pl.ds(start, MSG_ROWS)]

    def remote(k):
        target_pair, target_half, src = message(k)
        return pltpu.make_async_remote_copy(
            src_ref=src,
            dst_ref=own_ref.at[me, pl.ds(0, MSG_ROWS)],
            send_sem=send_sem.at[k],
            recv_sem=own_sem.at[me],
            device_id=(target_pair * 2 + half, target_half),
            device_id_type=MESH,
        )

    def local():
        _, _, src = message(0)
        return pltpu.make_async_copy(src, own_ref.at[me, pl.ds(0, MSG_ROWS)], own_sem.at[me])

    @pl.when(core == half)
    def _():
        local().start()

    @pl.when(core != half)
    def _():
        remote(0).start()

    def send(k, carry):
        remote(k).start()
        return carry

    lax.fori_loop(1, GROUPS, send, 0)

    def passing(g):
        return pltpu.make_async_remote_copy(
            src_ref=own_ref.at[g, pl.ds(0, MSG_ROWS)],
            dst_ref=other_ref.at[g, pl.ds(0, MSG_ROWS)],
            send_sem=pass_sem.at[g],
            recv_sem=other_sem.at[g],
            device_id=(pair * 2 + 1 - core, half),
            device_id_type=MESH,
        )

    def slot(j):
        return lax.bitwise_xor(me, j)

    def forward(j, carry):
        g = slot(j)
        ref = own_ref.at[g, pl.ds(0, MSG_ROWS)]
        pltpu.make_async_copy(ref, ref, own_sem.at[g]).wait()
        passing(g).start()
        return carry

    lax.fori_loop(0, GROUPS, forward, 0)

    @pl.when(core != half)
    def _():
        remote(0).wait_send()

    def finish_send(k, carry):
        remote(k).wait_send()
        return carry

    lax.fori_loop(1, GROUPS, finish_send, 0)

    def finish_pass(j, carry):
        passing(slot(j)).wait()
        return carry

    lax.fori_loop(0, GROUPS, finish_pass, 0)


def gather(tick_bars, prior_bars):
    tick = tick_bars.reshape(TICK_ROWS, 1, 128)
    prior = jnp.pad(prior_bars.reshape(-1), (GROUP_COLS, PAD_ROWS * 128 - GROUP_COLS - LEAD * GROUP_COLS))
    prior = prior.reshape(PAD_ROWS, 1, 128)
    slots = jax.ShapeDtypeStruct((GROUPS, SLOT_ROWS, 1, 128), jnp.float32)
    own, other = pl.pallas_call(
        gather_kernel,
        out_shape=(slots, slots),
        in_specs=[pl.BlockSpec(memory_space=pl.ANY)] * 2,
        out_specs=[pl.BlockSpec(memory_space=pl.ANY)] * 2,
        scratch_shapes=[
            pltpu.VMEM((SERIES_ROWS, 1, 128), jnp.float32),
            pltpu.SemaphoreType.DMA((3,)),
            pltpu.SemaphoreType.DMA((GROUPS,)),
            pltpu.SemaphoreType.DMA((GROUPS,)),
            pltpu.SemaphoreType.DMA((GROUPS,)),
            pltpu.SemaphoreType.DMA((GROUPS,)),
        ],
        compiler_params=pltpu.CompilerParams(collective_id=0, has_side_effects=True),
        name="gather_bars",
    )(tick, prior)
    return own.reshape(GROUPS, SLOT_ROWS, 128), other.reshape(GROUPS, SLOT_ROWS, 128)


def magnitudes(lhs, rhs):
    return jnp.abs(
        lax.dot_general(lhs, rhs, (((1,), (0,)), ((), ())), preferred_element_type=jnp.float32)
    )


def fold_rows(a):
    return jnp.sum(a.reshape(a.shape[0] // 8, 8, a.shape[1]), axis=0)


def unpack_bars(raw_ref, bars, half):
    low = lax.broadcasted_iota(jnp.int32, (SLOT_ROWS, 128), 1) < GROUP_COLS

    def aligned(p, carry):
        a, b = raw_ref[2 * p], raw_ref[2 * p + 1]
        cols = pl.ds(pl.multiple_of(p * 128, 128), 128)
        bars[0, :, cols] = jnp.where(low, a, pltpu.roll(b, GROUP_COLS, 1))
        bars[1, :, cols] = jnp.where(low, pltpu.roll(a, GROUP_COLS, 1), b)
        return carry

    def shifted(p, carry):
        a, b = raw_ref[2 * p], raw_ref[2 * p + 1]
        cols = pl.ds(pl.multiple_of(p * 128, 128), 128)
        bars[0, :, cols] = jnp.where(low, pltpu.roll(a, GROUP_COLS, 1), b)
        even = jnp.where(low, a, pltpu.roll(b, GROUP_COLS, 1))
        bars[1, :, cols] = pltpu.roll(even, SLOT_ROWS - 1, 0)
        return carry

    @pl.when(half == 1)
    def _():
        lax.fori_loop(0, GROUPS // 2, aligned, 0, unroll=4)

    @pl.when(half == 0)
    def _():
        lax.fori_loop(0, GROUPS // 2, shifted, 0, unroll=4)


def standardize(bars, scaled, width=512):
    valid = lax.broadcasted_iota(jnp.int32, (16, width), 0) < SPAN // 2

    def chunk(j, carry):
        cols = pl.ds(pl.multiple_of(j * width, width), width)
        for w in range(WIN_DEV):
            first = w * STRIDE
            even = jnp.where(valid, bars[0, pl.ds((first + 1) // 2, 16), cols], 0.0)
            odd = jnp.where(valid, bars[1, pl.ds(first // 2, 16), cols], 0.0)
            mean = (jnp.sum(even, axis=0, keepdims=True) + jnp.sum(odd, axis=0, keepdims=True)) * (1.0 / SPAN)
            even = jnp.where(valid, even - mean, 0.0)
            odd = jnp.where(valid, odd - mean, 0.0)
            squares = jnp.sum(even * even, axis=0, keepdims=True) + jnp.sum(odd * odd, axis=0, keepdims=True)
            scale = lax.rsqrt(jnp.maximum(squares, FLOOR_SQUARES))
            scaled[pl.ds(32 * w, 16), cols] = (even * scale).astype(jnp.bfloat16)
            scaled[pl.ds(32 * w + 16, 16), cols] = (odd * scale).astype(jnp.bfloat16)
        return carry

    lax.fori_loop(0, TILE // width, chunk, 0)
    scaled[pl.ds(96, 32), :] = jnp.zeros((32, scaled.shape[1]), jnp.bfloat16)


def connect_kernel(own_raw, other_raw, out_ref, bars, own, other, lhs_ref, rows, row_line, own_cols, other_cols):
    _, core, half = place()
    unpack_bars(own_raw, bars, half)
    standardize(bars, own)
    unpack_bars(other_raw, bars, half)
    standardize(bars, other)
    own[:, TILE:EXT] = own[:, 0:HALF]
    lane = lax.broadcasted_iota(jnp.int32, (128, 128), 1)

    def transpose_block(p, carry):
        at = pl.ds(pl.multiple_of(p * 128, 128), 128)
        turned = own[:, at].T
        for w in range(WIN_DEV):
            keep = (lane // 32 == w).astype(jnp.float32).astype(jnp.bfloat16)
            lhs_ref[w, at, :] = turned * keep
        return carry

    lax.fori_loop(0, TILE // 128, transpose_block, 0, unroll=2)
    own_cols[...] = jnp.zeros_like(own_cols)
    other_cols[...] = jnp.zeros_like(other_cols)

    def within(i, carry):
        row0 = pl.multiple_of(i * BLOCK, BLOCK)
        for w in range(WIN_DEV):
            lhs = lhs_ref[w, pl.ds(row0, BLOCK), :]
            total = None
            for d in range(0, HALF, BLOCK):
                cols = pl.ds(pl.multiple_of(row0 + d, BLOCK), BLOCK)
                a = magnitudes(lhs, own[:, cols])
                part = a[:, :128] + a[:, 128:]
                total = part if total is None else total + part
                if d:
                    own_cols[w, :, cols] += fold_rows(a)
            rows[w, pl.ds(row0, BLOCK), :] = total
            low = lax.rem(i, 8)
            across = pl.ds(pl.multiple_of(low * BLOCK + (i // 8) * 128, 128), 128)
            cols = pl.ds(pl.multiple_of((low + 8) * BLOCK, BLOCK), BLOCK)
            a = magnitudes(lhs_ref[w, across, :], own[:, cols])
            rows[w, across, :] += a[:, :128] + a[:, 128:]
            own_cols[w, :, cols] += fold_rows(a)
        return carry

    lax.fori_loop(0, TILE // BLOCK, within, 0, unroll=UNROLL)

    def between(i, carry):
        row0 = pl.multiple_of(i * BLOCK, BLOCK)
        col0 = lax.rem(i // 8 + core, 2) * HALF
        for w in range(WIN_DEV):
            lhs = lhs_ref[w, pl.ds(row0, BLOCK), :]
            total = rows[w, pl.ds(row0, BLOCK), :]
            for d in range(0, HALF, BLOCK):
                cols = pl.ds(pl.multiple_of(col0 + d, BLOCK), BLOCK)
                a = magnitudes(lhs, other[:, cols])
                total = total + (a[:, :128] + a[:, 128:])
                other_cols[w, :, cols] += fold_rows(a)
            for q in range(0, BLOCK, 128):
                line = jnp.sum(total[q : q + 128].T, axis=0, keepdims=True)
                row_line[pl.ds(w, 1), pl.ds(pl.multiple_of(row0 + q, 128), 128)] = line
        return carry

    lax.fori_loop(0, TILE // BLOCK, between, 0, unroll=UNROLL)
    scale = math.sqrt(SPAN) / ASSETS
    for w in range(WIN_DEV):
        one = pl.ds(w, 1)
        out_ref[1, one, :] = jnp.sum(other_cols[w], axis=0, keepdims=True) * scale
        mine = row_line[one, :] + jnp.sum(own_cols[w, :, 0:TILE], axis=0, keepdims=True)
        out_ref[0, one, HALF:TILE] = mine[:, HALF:] * scale
        wrapped = jnp.sum(own_cols[w, :, TILE:EXT], axis=0, keepdims=True)
        out_ref[0, one, 0:HALF] = (mine[:, :HALF] + wrapped) * scale


def connect(own_raw, other_raw):
    return pl.pallas_call(
        connect_kernel,
        out_shape=jax.ShapeDtypeStruct((2, WIN_DEV, TILE), jnp.float32),
        in_specs=[pl.BlockSpec(memory_space=pltpu.VMEM)] * 2,
        out_specs=pl.BlockSpec(memory_space=pltpu.VMEM),
        scratch_shapes=[
            pltpu.VMEM((2, SLOT_ROWS, TILE), jnp.float32),
            pltpu.VMEM((128, EXT), jnp.bfloat16),
            pltpu.VMEM((128, TILE), jnp.bfloat16),
            pltpu.VMEM((WIN_DEV, TILE, 128), jnp.bfloat16),
            pltpu.VMEM((WIN_DEV, TILE, 128), jnp.float32),
            pltpu.VMEM((8, TILE), jnp.float32),
            pltpu.VMEM((WIN_DEV, 8, EXT), jnp.float32),
            pltpu.VMEM((WIN_DEV, 8, TILE), jnp.float32),
        ],
        compiler_params=pltpu.CompilerParams(vmem_limit_bytes=48 * 2**20),
        name="connect",
    )(own_raw, other_raw)


def shards(tick_bars, prior_bars):
    own_raw, other_raw = gather(tick_bars, prior_bars)
    sums = connect(own_raw, other_raw)
    main = [(4 * pair + 2 * core + half, 4 * pair + 2 * half + core) for pair in range(32) for core in range(2) for half in range(2)]
    side = [(4 * pair + 2 * core + half, 4 * pair + 2 * half + 1 - core) for pair in range(32) for core in range(2) for half in range(2)]
    first = lax.ppermute(sums[0], ("tm", "asset"), main)
    second = lax.ppermute(sums[1], ("tm", "asset"), side)
    return first + second


def solution(mesh):
    in_specs = (P("asset", "tm", None), P("asset", "tm", None))
    out_specs = P("tm", "asset")
    return jax.shard_map(shards, mesh=mesh, in_specs=in_specs, out_specs=out_specs, check_vma=False)
```

time: 134 us -> 75.3 us (0.56)
  the two profiles are of different devices: /device:TPU:8 before, /device:TPU:1 now
where the time goes in v1:
time: 75.3 us; the launch traced here: 75.1 us
  Pallas kernels  63.5 us (84%)
  waiting for transfers between devices  4.45 us (6%)
  local copies, waits for them, and re-layouts  2.96 us (4%)
  starting transfers between devices  2.84 us (4%)
  other arithmetic  1.36 us (2%)
    pallas_call x1, Pallas kernels, connect(): pl.pallas_call(connect_kernel, out_shape=jax.ShapeDtypeStruct((2, WIN_DEV...  35.4 us
    pallas_call x1, Pallas kernels, gather(): pl.pallas_call(gather_kernel, out_shape=(slots, slots), in_specs=[pl.Bloc...  28 us
    ppermute x1, starting transfers between devices, shards(): first = lax.ppermute(sums[0], ('tm', 'asset'), main)  2.62 us
    ppermute x1, waiting for transfers between devices, shards(): first = lax.ppermute(sums[0], ('tm', 'asset'), main)  2.59 us
    unnamed x4, local copies, waits for them, and re-layouts  2.26 us
    ppermute x1, waiting for transfers between devices, shards(): second = lax.ppermute(sums[1], ('tm', 'asset'), side)  1.85 us
  transfers between devices with their start and end apart: 2, of which 2 were waited for; matrix products, arithmetic and copies ran while one was open for 0% of the time, Pallas kernels for 0%

profile of v1, /device:TPU:1, one launch (start us, length us, event | category | flops | bytes accessed | tf_op | source)
XLA Modules:
  0.0 75.1 jit_solution(10512855399638322813)
XLA Ops:
  0.0 0.7 reduce
  0.7 0.7 pad.4
  1.4 28.0 %gather_bars.1 = (f32[64,24,1,128]{3,2,1,0:T(1,128)}, f32[64,24,1,128]{3,2,1,0:T(1,128)}) custom-call(f32[480,1,128]{2,1,0:T(1,128)} %bitcast.10, f32[16,1,128]{2,1,0:T(1,128)} %bitcast.11), custom_call_target="tpu_custom_call" | custom-call | tf_op jit(solution)/shard_map/gather_bars/pallas_call | solution.py:149
  29.4 0.0 copy-start
  29.5 1.1 %copy-done = f32[64,24,1,128]{3,2,1,0:T(1,128)S(1)} copy-done((f32[64,24,1,128]{3,2,1,0:T(1,128)S(1)}, f32[64,24,1,128]{3,2,1,0:T(1,128)}, u32[]{:S(2)}) %copy-start) | copy-done | bytes 786456
  30.6 0.0 copy-start.1
  30.6 1.1 %copy-done.1 = f32[64,24,1,128]{3,2,1,0:T(1,128)S(1)} copy-done((f32[64,24,1,128]{3,2,1,0:T(1,128)S(1)}, f32[64,24,1,128]{3,2,1,0:T(1,128)}, u32[]{:S(2)}) %copy-start.1) | copy-done | bytes 786456
  31.7 35.4 %connect.1 = f32[2,3,4096]{2,1,0:T(4,128)S(1)} custom-call(f32[64,24,128]{2,1,0:T(8,128)S(1)} %bitcast.8, f32[64,24,128]{2,1,0:T(8,128)S(1)} %bitcast.9), custom_call_target="tpu_custom_call" | custom-call | tf_op jit(solution)/shard_map/connect/pallas_call | solution.py:299
  67.2 0.2 collective-permute-start.1
  67.4 2.6 %collective-permute-start = (f32[3,4096]{1,0:T(4,128)S(1)}, f32[3,4096]{1,0:T(4,128)S(1)}, u32[]{:S(2)}, u32[]{:S(2)}) collective-permute-start(f32[3,4096]{1,0:T(4,128)S(1)} %get-tuple-element.10), channel_id=1, source_target_pairs={{0,0},{1,2},{2,1},{3,3},{4,4},{5,6},{6,5},{7,7},{8,8},{9,10},{10,9... | collective-permute-start | bytes 147464 | tf_op jit(solution)/shard_map/ppermute | solution.py:324
  70.0 1.9 %collective-permute-done.1 = f32[3,4096]{1,0:T(4,128)S(1)} collective-permute-done((f32[3,4096]{1,0:T(4,128)S(1)}, f32[3,4096]{1,0:T(4,128)S(1)}, u32[]{:S(2)}, u32[]{:S(2)}) %collective-permute-start.1) | collective-permute-done | bytes 49184 | tf_op jit(solution)/shard_map/ppermute | solution.py:325
  71.9 2.6 %collective-permute-done = f32[3,4096]{1,0:T(4,128)S(1)} collective-permute-done((f32[3,4096]{1,0:T(4,128)S(1)}, f32[3,4096]{1,0:T(4,128)S(1)}, u32[]{:S(2)}, u32[]{:S(2)}) %collective-permute-start) | collective-permute-done | bytes 49184 | tf_op jit(solution)/shard_map/ppermute | solution.py:324
  74.5 0.6 add.5
  (1 shorter events, 0.0 us)
Async XLA Ops:
  29.4 1.1 %copy-start = (f32[64,24,1,128]{3,2,1,0:T(1,128)S(1)}, f32[64,24,1,128]{3,2,1,0:T(1,128)}, u32[]{:S(2)}) copy-start(f32[64,24,1,128]{3,2,1,0:T(1,128)} %get-tuple-element.7) | copy-start | bytes 2359300
  30.6 1.1 %copy-start.1 = (f32[64,24,1,128]{3,2,1,0:T(1,128)S(1)}, f32[64,24,1,128]{3,2,1,0:T(1,128)}, u32[]{:S(2)}) copy-start(f32[64,24,1,128]{3,2,1,0:T(1,128)} %get-tuple-element.8) | copy-start | bytes 2359300
  67.2 4.7 %collective-permute-start.1 = (f32[3,4096]{1,0:T(4,128)S(1)}, f32[3,4096]{1,0:T(4,128)S(1)}, u32[]{:S(2)}, u32[]{:S(2)}) collective-permute-start(f32[3,4096]{1,0:T(4,128)S(1)} %get-tuple-element.9), channel_id=1, source_target_pairs={{0,1},{1,3},{2,0},{3,2},{4,5},{5,7},{6,4},{7,6},{8,9},{9,11},{10,8... | collective-permute-start | bytes 147464 | tf_op jit(solution)/shard_map/ppermute | solution.py:325
  67.4 7.1 %collective-permute-start = (f32[3,4096]{1,0:T(4,128)S(1)}, f32[3,4096]{1,0:T(4,128)S(1)}, u32[]{:S(2)}, u32[]{:S(2)}) collective-permute-start(f32[3,4096]{1,0:T(4,128)S(1)} %get-tuple-element.10), channel_id=1, source_target_pairs={{0,0},{1,2},{2,1},{3,3},{4,4},{5,6},{6,5},{7,7},{8,8},{9,10},{10,9... | collective-permute-start | bytes 147464 | tf_op jit(solution)/shard_map/ppermute | solution.py:324

commit v2 on v1

v2 whole, which is shorter than its diff:
```python
import functools
import math

import jax
import jax.numpy as jnp
from jax import lax
from jax.experimental import pallas as pl
from jax.experimental.pallas import tpu as pltpu
from jax.sharding import PartitionSpec as P

ASSETS = 8192
SPAN = 30
STRIDE = 5
WIN_DEV = 3
LEAD = 25
FLOOR_SQUARES = 1.0

MESH = pl.DeviceIdType.MESH
TILE = ASSETS // 2
GROUPS = 64
GROUP_COLS = TILE // GROUPS
BLOCK_BARS = WIN_DEV * STRIDE
LEAD_ROWS = 13
TICK_ROWS = 480
SERIES_ROWS = LEAD_ROWS + TICK_ROWS + 1
MSG_ROWS = 21
SLOT_ROWS = 24
BLOCK = 256
HALF = TILE // 2
EXT = TILE + HALF
UNROLL = 4


def place():
    tm = lax.axis_index("tm")
    return tm // 2, lax.rem(tm, 2), lax.axis_index("asset")


def magnitudes(lhs, rhs):
    return jnp.abs(
        lax.dot_general(lhs, rhs, (((1,), (0,)), ((), ())), preferred_element_type=jnp.float32)
    )


def fold_rows(a):
    return jnp.sum(a.reshape(a.shape[0] // 8, 8, a.shape[1]), axis=0)


def prepare(raw_ref, bars, scaled, chunk, half):
    low = lax.broadcasted_iota(jnp.int32, (SLOT_ROWS, 128), 1) < GROUP_COLS
    for p in range(4):
        slot = chunk * 8 + 2 * p
        a, b = raw_ref[slot, :, 0, :], raw_ref[slot + 1, :, 0, :]
        cols = pl.ds(p * 128, 128)
        even = jnp.where(low, a, pltpu.roll(b, GROUP_COLS, 1))
        odd = jnp.where(low, pltpu.roll(a, GROUP_COLS, 1), b)
        aligned = half == 1
        bars[0, :, cols] = jnp.where(aligned, even, odd)
        bars[1, :, cols] = jnp.where(aligned, odd, pltpu.roll(even, SLOT_ROWS - 1, 0))
    valid = lax.broadcasted_iota(jnp.int32, (16, 512), 0) < SPAN // 2
    at = pl.ds(pl.multiple_of(chunk * 512, 512), 512)
    for w in range(WIN_DEV):
        first = w * STRIDE
        even = jnp.where(valid, bars[0, pl.ds((first + 1) // 2, 16), :], 0.0)
        odd = jnp.where(valid, bars[1, pl.ds(first // 2, 16), :], 0.0)
        mean = (jnp.sum(even, axis=0, keepdims=True) + jnp.sum(odd, axis=0, keepdims=True)) * (1.0 / SPAN)
        even = jnp.where(valid, even - mean, 0.0)
        odd = jnp.where(valid, odd - mean, 0.0)
        squares = jnp.sum(even * even, axis=0, keepdims=True) + jnp.sum(odd * odd, axis=0, keepdims=True)
        scale = lax.rsqrt(jnp.maximum(squares, FLOOR_SQUARES))
        scaled[pl.ds(32 * w, 16), at] = (even * scale).astype(jnp.bfloat16)
        scaled[pl.ds(32 * w + 16, 16), at] = (odd * scale).astype(jnp.bfloat16)


def turn(scaled, lhs_ref, chunk):
    lane = lax.broadcasted_iota(jnp.int32, (128, 128), 1)
    for p in range(4):
        at = pl.ds(pl.multiple_of(chunk * 512 + p * 128, 128), 128)
        turned = scaled[:, at].T
        for w in range(WIN_DEV):
            keep = (lane // 32 == w).astype(jnp.float32).astype(jnp.bfloat16)
            lhs_ref[w, at, :] = turned * keep


def kernel(
    tick_ref, prior_ref, out_ref, series, own_raw, other_raw, bars, own, other, lhs_ref, rows, own_cols, other_cols, result, arrived,
    load_sem, send_sem, pass_sem, own_sem, other_sem, result_send, result_recv,
):
    pair, core, half = place()
    me = pair * 2 + core
    sibling = pair * 2 + 1 - core
    load = pltpu.make_async_copy(tick_ref, series.at[pl.ds(LEAD_ROWS, TICK_ROWS)], load_sem)
    load.start()

    barrier = pltpu.get_barrier_semaphore()

    def greet(g, carry):
        @pl.when(jnp.logical_or(g != me, core != half))
        def _():
            pl.semaphore_signal(barrier, inc=1, device_id=(g, core), device_id_type=MESH)

        return carry

    lax.fori_loop(0, GROUPS, greet, 0)
    pl.semaphore_signal(barrier, inc=1, device_id=(sibling, half), device_id_type=MESH)

    low = lax.broadcasted_iota(jnp.int32, (1, 128), 1) < GROUP_COLS
    before = jnp.zeros((1, 128), jnp.float32)
    for r in range(LEAD_ROWS):
        now = pltpu.roll(prior_ref[pl.ds(r, 1), :], GROUP_COLS, 1)
        series[r] = jnp.where(low, before, now)
        before = now
    series[LEAD_ROWS + TICK_ROWS] = jnp.zeros((1, 128), jnp.float32)
    own[pl.ds(96, 32), :] = jnp.zeros((32, TILE), jnp.bfloat16)
    other[pl.ds(96, 32), :] = jnp.zeros((32, TILE), jnp.bfloat16)
    own_cols[...] = jnp.zeros_like(own_cols)
    other_cols[...] = jnp.zeros_like(other_cols)

    pl.semaphore_wait(barrier, GROUPS + jnp.where(core == half, 0, 1))
    load.wait()

    def message(k):
        target_pair = lax.bitwise_xor(pair, k // 2)
        target_half = lax.bitwise_xor(half, lax.rem(k, 2))
        start = (BLOCK_BARS * (2 * target_pair + target_half) + 1) // 2
        return target_pair, target_half, series.at[pl.ds(start, MSG_ROWS)]

    def remote(k):
        target_pair, target_half, src = message(k)
        return pltpu.make_async_remote_copy(
            src_ref=src,
            dst_ref=own_raw.at[me, pl.ds(0, MSG_ROWS)],
            send_sem=send_sem.at[k],
            recv_sem=own_sem.at[me],
            device_id=(target_pair * 2 + half, target_half),
            device_id_type=MESH,
        )

    @pl.when(core == half)
    def _():
        _, _, src = message(0)
        pltpu.make_async_copy(src, own_raw.at[me, pl.ds(0, MSG_ROWS)], own_sem.at[me]).start()

    @pl.when(core != half)
    def _():
        remote(0).start()

    def send(k, carry):
        remote(k).start()
        return carry

    lax.fori_loop(1, GROUPS, send, 0)

    def passing(g):
        return pltpu.make_async_remote_copy(
            src_ref=own_raw.at[g, pl.ds(0, MSG_ROWS)],
            dst_ref=other_raw.at[g, pl.ds(0, MSG_ROWS)],
            send_sem=pass_sem.at[g],
            recv_sem=other_sem.at[g],
            device_id=(sibling, half),
            device_id_type=MESH,
        )

    def receive(q, carry):
        chunk = lax.bitwise_xor(me // 8, q)
        for j in range(8):
            g = chunk * 8 + j
            ref = own_raw.at[g, pl.ds(0, MSG_ROWS)]
            pltpu.make_async_copy(ref, ref, own_sem.at[g]).wait()
            passing(g).start()
        prepare(own_raw, bars, own, chunk, half)
        turn(own, lhs_ref, chunk)
        return carry

    first_half = me // 32

    def square(h):
        base = h * 8

        def step(i, carry):
            row0 = pl.multiple_of((base + i) * BLOCK, BLOCK)
            for w in range(WIN_DEV):
                lhs = lhs_ref[w, pl.ds(row0, BLOCK), :]
                total = None
                for d in range(4):
                    cols = pl.ds(pl.multiple_of((base + lax.rem(i + d, 8)) * BLOCK, BLOCK), BLOCK)
                    a = magnitudes(lhs, own[:, cols])
                    part = a[:, :128] + a[:, 128:]
                    total = part if total is None else total + part
                    if d:
                        own_cols[w, :, cols] += fold_rows(a)
                rows[w, pl.ds(row0, BLOCK), :] = total
                near = lax.rem(i, 4)
                across = pl.ds(pl.multiple_of((base + near) * BLOCK + (i // 4) * 128, 128), 128)
                cols = pl.ds(pl.multiple_of((base + near + 4) * BLOCK, BLOCK), BLOCK)
                a = magnitudes(lhs_ref[w, across, :], own[:, cols])
                rows[w, across, :] += a[:, :128] + a[:, 128:]
                own_cols[w, :, cols] += fold_rows(a)
            return carry

        lax.fori_loop(0, 8, step, 0, unroll=UNROLL)

    def stage(s, carry):
        lax.fori_loop(4 * s, 4 * s + 4, receive, 0)
        square(lax.bitwise_xor(first_half, s))
        return carry

    lax.fori_loop(0, 2, stage, 0)

    def across_halves(i, carry):
        row0 = pl.multiple_of(i * BLOCK, BLOCK)
        for w in range(WIN_DEV):
            lhs = lhs_ref[w, pl.ds(row0, BLOCK), :]
            total = rows[w, pl.ds(row0, BLOCK), :]
            for d in range(HALF, TILE, BLOCK):
                cols = pl.ds(d, BLOCK)
                a = magnitudes(lhs, own[:, cols])
                total = total + (a[:, :128] + a[:, 128:])
                own_cols[w, :, cols] += fold_rows(a)
            rows[w, pl.ds(row0, BLOCK), :] = total
        return carry

    lax.fori_loop(0, HALF // BLOCK, across_halves, 0, unroll=UNROLL)

    def receive_other(q, carry):
        chunk = lax.bitwise_xor(me // 8, q)
        for j in range(8):
            passing(chunk * 8 + j).wait()
        prepare(other_raw, bars, other, chunk, half)
        return carry

    lax.fori_loop(0, 8, receive_other, 0)

    def across_tiles(i, carry):
        row0 = pl.multiple_of(i * BLOCK, BLOCK)
        col0 = lax.rem(i // 8 + core, 2) * HALF
        for w in range(WIN_DEV):
            lhs = lhs_ref[w, pl.ds(row0, BLOCK), :]
            total = rows[w, pl.ds(row0, BLOCK), :]
            for d in range(0, HALF, BLOCK):
                cols = pl.ds(pl.multiple_of(col0 + d, BLOCK), BLOCK)
                a = magnitudes(lhs, other[:, cols])
                total = total + (a[:, :128] + a[:, 128:])
                other_cols[w, :, cols] += fold_rows(a)
            for q in range(0, BLOCK, 128):
                line = jnp.sum(total[q : q + 128].T, axis=0, keepdims=True)
                result[0, pl.ds(w, 1), pl.ds(pl.multiple_of(row0 + q, 128), 128)] = line
        return carry

    lax.fori_loop(0, TILE // BLOCK, across_tiles, 0, unroll=UNROLL)
    scale = math.sqrt(SPAN) / ASSETS
    for w in range(WIN_DEV):
        one = pl.ds(w, 1)
        result[1, one, :] = jnp.sum(other_cols[w], axis=0, keepdims=True) * scale
        result[0, one, :] = (result[0, one, :] + jnp.sum(own_cols[w], axis=0, keepdims=True)) * scale

    def result_copy(which):
        tile = core if which == 0 else 1 - core
        return pltpu.make_async_remote_copy(
            src_ref=result.at[which],
            dst_ref=arrived.at[which],
            send_sem=result_send.at[which],
            recv_sem=result_recv.at[which],
            device_id=(pair * 2 + half, tile),
            device_id_type=MESH,
        )

    result_copy(1).start()

    @pl.when(core != half)
    def _():
        result_copy(0).start()

    def finish_send(k, carry):
        remote(k).wait_send()
        return carry

    @pl.when(core != half)
    def _():
        remote(0).wait_send()

    lax.fori_loop(1, GROUPS, finish_send, 0)
    result_copy(1).wait()

    @pl.when(core != half)
    def _():
        result_copy(0).wait()
        out_ref[...] = arrived[0] + arrived[1]

    @pl.when(core == half)
    def _():
        out_ref[...] = result[0] + arrived[1]


def shards(tick_bars, prior_bars):
    slots = pltpu.VMEM((GROUPS, SLOT_ROWS, 1, 128), jnp.float32)
    prior = jnp.pad(prior_bars.reshape(1, -1), ((0, 0), (0, LEAD_ROWS * 128 - LEAD * GROUP_COLS))).reshape(LEAD_ROWS, 128)
    return pl.pallas_call(
        kernel,
        out_shape=jax.ShapeDtypeStruct((WIN_DEV, TILE), jnp.float32),
        in_specs=[pl.BlockSpec(memory_space=pl.ANY), pl.BlockSpec(memory_space=pltpu.VMEM)],
        out_specs=pl.BlockSpec(memory_space=pltpu.VMEM),
        scratch_shapes=[
            pltpu.VMEM((SERIES_ROWS, 1, 128), jnp.float32),
            slots,
            slots,
            pltpu.VMEM((2, SLOT_ROWS, 512), jnp.float32),
            pltpu.VMEM((128, TILE), jnp.bfloat16),
            pltpu.VMEM((128, TILE), jnp.bfloat16),
            pltpu.VMEM((WIN_DEV, TILE, 128), jnp.bfloat16),
            pltpu.VMEM((WIN_DEV, TILE, 128), jnp.float32),
            pltpu.VMEM((WIN_DEV, 8, TILE), jnp.float32),
            pltpu.VMEM((WIN_DEV, 8, TILE), jnp.float32),
            pltpu.VMEM((2, WIN_DEV, TILE), jnp.float32),
            pltpu.VMEM((2, WIN_DEV, TILE), jnp.float32),
            pltpu.SemaphoreType.DMA,
            pltpu.SemaphoreType.DMA((GROUPS,)),
            pltpu.SemaphoreType.DMA((GROUPS,)),
            pltpu.SemaphoreType.DMA((GROUPS,)),
            pltpu.SemaphoreType.DMA((GROUPS,)),
            pltpu.SemaphoreType.DMA((2,)),
            pltpu.SemaphoreType.DMA((2,)),
        ],
        compiler_params=pltpu.CompilerParams(collective_id=0, has_side_effects=True, vmem_limit_bytes=56 * 2**20),
        name="connect",
    )(tick_bars.reshape(TICK_ROWS, 1, 128), prior)


def solution(mesh):
    in_specs = (P("asset", "tm", None), P("asset", "tm", None))
    out_specs = P("tm", "asset")
    return jax.shard_map(shards, mesh=mesh, in_specs=in_specs, out_specs=out_specs, check_vma=False)
```

time: 75.3 us -> 62 us (0.82)
  Pallas kernels: 63.5 us -> 59 us
  waiting for transfers between devices: 4.45 us -> 0 us
  starting transfers between devices: 2.84 us -> 0 us
  other arithmetic: 1.36 us -> 0 us
    pallas_call x2 -> x1, Pallas kernels: 63.5 us -> 59 us  [shards(): pl.pallas_call(kernel, out_shape=jax.ShapeDtypeStruct((WIN_DEV, TILE), jn...]
    ppermute x2 -> x0, waiting for transfers between devices: 4.45 us -> none  [the longest x1 2.59 us: shards(): first = lax.ppermute(sums[0], ('tm', 'asset'), main)]
    ppermute x2 -> x0, starting transfers between devices: 2.84 us -> none  [the longest x1 2.62 us: shards(): first = lax.ppermute(sums[0], ('tm', 'asset'), main)]
    unnamed x4 -> x1, local copies, waits for them, and re-layouts: 2.26 us -> 1.48 us
  transfers between devices with their start and end apart: 2 -> 0, of which waited for: 2 -> 0; matrix products, arithmetic and copies ran while one was open for 0% -> 0% of each run, Pallas kernels for 0% -> 0%
where the time goes in v2:
time: 62 us; the launch traced here: 61.8 us
  Pallas kernels  59 us (95%)
  local copies, waits for them, and re-layouts  2.79 us (4%)
    pallas_call x1, Pallas kernels, shards(): pl.pallas_call(kernel, out_shape=jax.ShapeDtypeStruct((WIN_DEV, TILE), jn...  59 us
    unnamed x1, local copies, waits for them, and re-layouts  1.48 us
    pad x1, local copies, waits for them, and re-layouts, shards(): jnp.pad(prior_bars.reshape(1, -1), ((0, 0), (0, LEAD_ROWS * 128 - LEAD *...  1.31 us

profile of v2, /device:TPU:1, one launch (start us, length us, event | category | flops | bytes accessed | tf_op | source)
XLA Modules:
  0.0 61.8 jit_solution(10969743642168482648)
XLA Ops:
  0.0 1.3 %pad_reduce_fusion = f32[1664]{0:T(1024)} fusion(f32[1,1600]{1,0:T(1,128)} %bitcast.5), kind=kLoop, calls=%fused_computation | loop fusion | bytes 13056 | tf_op jit(solution)/shard_map/jit(_pad)/pad | solution.py:297
  1.3 59.0 %connect.1 = f32[3,4096]{1,0:T(4,128)} custom-call(f32[480,1,128]{2,1,0:T(1,128)} %bitcast.3, f32[13,128]{1,0:T(8,128)} %bitcast.4), custom_call_target="tpu_custom_call" | custom-call | tf_op jit(solution)/shard_map/connect/pallas_call | solution.py:298
  60.3 1.5 %copy.4 = f32[3,4096]{1,0:T(4,128)} copy(f32[3,4096]{1,0:T(4,128)} %connect.1) | data formatting | bytes 98304

commit v3 on v2

v3 whole, which is shorter than its diff:
```python
import functools
import math

import jax
import jax.numpy as jnp
from jax import lax
from jax.experimental import pallas as pl
from jax.experimental.pallas import tpu as pltpu
from jax.sharding import PartitionSpec as P

ASSETS = 8192
SPAN = 30
STRIDE = 5
WIN_DEV = 3
LEAD = 25
FLOOR_SQUARES = 1.0

MESH = pl.DeviceIdType.MESH
TILE = ASSETS // 2
GROUPS = 64
GROUP_COLS = TILE // GROUPS
BLOCK_BARS = WIN_DEV * STRIDE
LEAD_ROWS = 13
TICK_ROWS = 480
SERIES_ROWS = LEAD_ROWS + TICK_ROWS + 1
MSG_ROWS = 21
SLOT_ROWS = 24
BLOCK = 256
HALF = TILE // 2
EXT = TILE + HALF
UNROLL = 4


def place():
    tm = lax.axis_index("tm")
    return tm // 2, lax.rem(tm, 2), lax.axis_index("asset")


def magnitudes(lhs, rhs):
    return jnp.abs(
        lax.dot_general(lhs, rhs, (((1,), (0,)), ((), ())), preferred_element_type=jnp.float32)
    )


def fold_rows(a):
    return jnp.sum(a.reshape(a.shape[0] // 8, 8, a.shape[1]), axis=0)


def prepare(raw_ref, bars, scaled, lhs_ref, chunk, half):
    low = lax.broadcasted_iota(jnp.int32, (SLOT_ROWS, 128), 1) < GROUP_COLS
    valid = lax.broadcasted_iota(jnp.int32, (16, 128), 0) < SPAN // 2
    aligned = half == 1
    for p in range(4):
        slot = chunk * 8 + 2 * p
        a, b = raw_ref[slot, :, 0, :], raw_ref[slot + 1, :, 0, :]
        even = jnp.where(low, a, pltpu.roll(b, GROUP_COLS, 1))
        odd = jnp.where(low, pltpu.roll(a, GROUP_COLS, 1), b)
        bars[0, p] = jnp.where(aligned, even, odd)
        bars[1, p] = jnp.where(aligned, odd, pltpu.roll(even, SLOT_ROWS - 1, 0))
    for p in range(4):
        at = pl.ds(pl.multiple_of(chunk * 512 + p * 128, 128), 128)
        parts = []
        for w in range(WIN_DEV):
            first = w * STRIDE
            even = jnp.where(valid, bars[0, p, pl.ds((first + 1) // 2, 16), :], 0.0)
            odd = jnp.where(valid, bars[1, p, pl.ds(first // 2, 16), :], 0.0)
            mean = jnp.sum(even + odd, axis=0, keepdims=True) * (1.0 / SPAN)
            even = jnp.where(valid, even - mean, 0.0)
            odd = jnp.where(valid, odd - mean, 0.0)
            squares = jnp.sum(even * even + odd * odd, axis=0, keepdims=True)
            scale = lax.rsqrt(jnp.maximum(squares, FLOOR_SQUARES))
            even, odd = (even * scale).astype(jnp.bfloat16), (odd * scale).astype(jnp.bfloat16)
            scaled[w, pl.ds(32 * w, 16), at] = even
            scaled[w, pl.ds(32 * w + 16, 16), at] = odd
            parts += [even, odd]
        parts.append(jnp.zeros((32, 128), jnp.bfloat16))
        lhs_ref[at, :] = jnp.concatenate(parts, axis=0).T


def kernel(
    tick_ref, prior_ref, out_ref, series, prior, own_raw, bars, own, other, lhs_ref, rows, own_cols, other_cols, result, arrived,
    load_sem, send_sem, own_sem, pass_sem, other_sem, result_send, result_recv,
):
    pair, core, half = place()
    me = pair * 2 + core
    sibling = pair * 2 + 1 - core
    prior_load = pltpu.make_async_copy(prior_ref, prior, load_sem.at[0])
    prior_load.start()
    load = pltpu.make_async_copy(tick_ref, series.at[pl.ds(LEAD_ROWS, TICK_ROWS)], load_sem.at[1])
    load.start()

    barrier = pltpu.get_barrier_semaphore()

    def greet(j, carry):
        g = lax.bitwise_xor(me, GROUPS - 1 - j)

        @pl.when(jnp.logical_or(g != me, core != half))
        def _():
            pl.semaphore_signal(barrier, inc=1, device_id=(g, core), device_id_type=MESH)

        return carry

    lax.fori_loop(0, GROUPS, greet, 0)
    pl.semaphore_signal(barrier, inc=1, device_id=(sibling, half), device_id_type=MESH)

    prior_load.wait()
    low = lax.broadcasted_iota(jnp.int32, (1, 128), 1) < GROUP_COLS
    series[0] = jnp.where(low, 0.0, pltpu.roll(prior[:, 0:128], GROUP_COLS, 1))
    for r in range(1, LEAD_ROWS):
        series[r] = prior[:, 128 * r - GROUP_COLS : 128 * r + GROUP_COLS]
    series[LEAD_ROWS + TICK_ROWS] = jnp.zeros((1, 128), jnp.float32)
    own_cols[...] = jnp.zeros_like(own_cols)
    other_cols[...] = jnp.zeros_like(other_cols)

    def clear(i, carry):
        at = pl.ds(pl.multiple_of(i * 256, 256), 256)
        for w in range(WIN_DEV):
            rows[w, at, :] = jnp.zeros((256, 128), jnp.float32)
            for first, last in ((0, 32 * w), (32 * w + 32, 128)):
                if last > first:
                    own[w, pl.ds(first, last - first), at] = jnp.zeros((last - first, 256), jnp.bfloat16)
                    other[w, pl.ds(first, last - first), at] = jnp.zeros((last - first, 256), jnp.bfloat16)
        return carry

    lax.fori_loop(0, TILE // 256, clear, 0)
    pl.semaphore_wait(barrier, GROUPS + jnp.where(core == half, 0, 1))
    load.wait()

    def message(k):
        target_pair = lax.bitwise_xor(pair, k // 2)
        target_half = lax.bitwise_xor(half, lax.rem(k, 2))
        start = (BLOCK_BARS * (2 * target_pair + target_half) + 1) // 2
        return target_pair, target_half, series.at[pl.ds(start, MSG_ROWS)]

    def remote(k):
        target_pair, target_half, src = message(k)
        return pltpu.make_async_remote_copy(
            src_ref=src,
            dst_ref=own_raw.at[me, pl.ds(0, MSG_ROWS)],
            send_sem=send_sem.at[k],
            recv_sem=own_sem.at[me],
            device_id=(target_pair * 2 + half, target_half),
            device_id_type=MESH,
        )

    @pl.when(core == half)
    def _():
        _, _, src = message(0)
        pltpu.make_async_copy(src, own_raw.at[me, pl.ds(0, MSG_ROWS)], own_sem.at[me]).start()

    @pl.when(core != half)
    def _():
        remote(0).start()

    def send(k, carry):
        remote(k).start()
        return carry

    lax.fori_loop(1, GROUPS, send, 0)

    def passing(q, w):
        at = pl.ds(pl.multiple_of(lax.bitwise_xor(me // 8, q) * 512, 512), 512)
        return pltpu.make_async_remote_copy(
            src_ref=own.at[w, pl.ds(32 * w, 32), at],
            dst_ref=other.at[w, pl.ds(32 * w, 32), at],
            send_sem=pass_sem.at[q, w],
            recv_sem=other_sem.at[q, w],
            device_id=(sibling, half),
            device_id_type=MESH,
        )

    def pass_on(q):
        for w in range(WIN_DEV):
            passing(q, w).start()

    def receive(q):
        chunk = lax.bitwise_xor(me // 8, q)
        for j in range(8):
            g = chunk * 8 + j
            ref = own_raw.at[g, pl.ds(0, MSG_ROWS)]
            pltpu.make_async_copy(ref, ref, own_sem.at[g]).wait()
        prepare(own_raw, bars, own, lhs_ref, chunk, half)
        return chunk

    def block(i):
        return pl.ds(pl.multiple_of(i * BLOCK, BLOCK), BLOCK)

    def pairs(w, row_at, col_at, right, cols):
        a = magnitudes(lhs_ref[row_at, :], right[w, :, col_at])
        if cols is not None:
            cols[w, :, col_at] += fold_rows(a)
        return a[:, :128] + a[:, 128:]

    def early(q, carry):
        chunk = receive(q)

        def with_earlier(r, carry):
            left = lax.bitwise_xor(me // 8, r)
            for w in range(WIN_DEV):
                for i in range(2):
                    row_at = block(2 * chunk + i)
                    rows[w, row_at, :] += pairs(w, row_at, block(2 * left), own, own_cols) + pairs(
                        w, row_at, block(2 * left + 1), own, own_cols
                    )
            return carry

        first, second = block(2 * chunk), block(2 * chunk + 1)
        for w in range(WIN_DEV):
            rows[w, first, :] += pairs(w, first, first, own, None) + pairs(w, first, second, own, own_cols)
            rows[w, second, :] += pairs(w, second, second, own, None)
        pass_on(q)
        lax.fori_loop(0, q, with_earlier, 0)
        return carry

    lax.fori_loop(0, 4, early, 0)
    first_half = me // 32
    near, far = first_half * 8, 8 - first_half * 8

    def late(q, carry):
        chunk = receive(q)
        for i in range(2):
            row_at = block(2 * chunk + i)
            for w in range(WIN_DEV):
                total = rows[w, row_at, :]
                for d in range(8):
                    total = total + pairs(w, row_at, block(near + d), own, own_cols)
                rows[w, row_at, :] = total
        pass_on(q)
        return carry

    lax.fori_loop(4, 8, late, 0)

    def receive_other(q, carry):
        for w in range(WIN_DEV):
            passing(q, w).wait_recv()
        return carry

    def sum_rows(w, i, total):
        for q in range(0, BLOCK, 128):
            at = pl.ds(pl.multiple_of(i * BLOCK + q, 128), 128)
            result[0, pl.ds(w, 1), at] = jnp.sum(total[q : q + 128].T, axis=0, keepdims=True)

    def across_tiles(h, carry):
        lax.fori_loop(4 * h, 4 * h + 4, receive_other, 0)
        col_half = lax.bitwise_xor(first_half, h)
        row_half = lax.rem(col_half + core, 2)

        def step(i, carry):
            row_at = block(row_half * 8 + i)
            for w in range(WIN_DEV):
                total = rows[w, row_at, :]
                for d in range(8):
                    total = total + pairs(w, row_at, block(col_half * 8 + d), other, other_cols)
                rows[w, row_at, :] = total
                sum_rows(w, row_half * 8 + i, total)
            return carry

        lax.fori_loop(0, 8, step, 0, unroll=UNROLL)
        return carry

    lax.fori_loop(0, 2, across_tiles, 0)

    for i in range(8):
        row_at = block(far + i)
        low = i % 4
        half_at = pl.ds(pl.multiple_of((far + low) * BLOCK + (i // 4) * 128, 128), 128)
        for w in range(WIN_DEV):
            total = rows[w, row_at, :]
            for d in range(4):
                total = total + pairs(w, row_at, block(far + (i + d) % 8), own, own_cols if d else None)
            rows[w, row_at, :] = total
            rows[w, half_at, :] += pairs(w, half_at, block(far + low + 4), own, own_cols)
            if i >= 4:
                sum_rows(w, far + low, rows[w, block(far + low), :])
                sum_rows(w, far + i, rows[w, row_at, :])

    scale = math.sqrt(SPAN) / ASSETS
    for w in range(WIN_DEV):
        one = pl.ds(w, 1)
        result[1, one, :] = jnp.sum(other_cols[w], axis=0, keepdims=True) * scale
        result[0, one, :] = (result[0, one, :] + jnp.sum(own_cols[w], axis=0, keepdims=True)) * scale

    def result_copy(which):
        tile = core if which == 0 else 1 - core
        return pltpu.make_async_remote_copy(
            src_ref=result.at[which],
            dst_ref=arrived.at[which],
            send_sem=result_send.at[which],
            recv_sem=result_recv.at[which],
            device_id=(pair * 2 + half, tile),
            device_id_type=MESH,
        )

    result_copy(1).start()

    @pl.when(core != half)
    def _():
        result_copy(0).start()

    def finish_send(k, carry):
        remote(k).wait_send()
        return carry

    @pl.when(core != half)
    def _():
        remote(0).wait_send()

    lax.fori_loop(1, GROUPS, finish_send, 0)

    def finish_pass(q, carry):
        for w in range(WIN_DEV):
            passing(q, w).wait_send()
        return carry

    lax.fori_loop(0, 8, finish_pass, 0)
    result_copy(1).wait()
    out_ref[1] = arrived[1]

    @pl.when(core != half)
    def _():
        result_copy(0).wait()
        out_ref[0] = arrived[0]

    @pl.when(core == half)
    def _():
        out_ref[0] = result[0]


def shards(tick_bars, prior_bars):
    sums = pl.pallas_call(
        kernel,
        out_shape=jax.ShapeDtypeStruct((2, WIN_DEV, TILE), jnp.float32),
        in_specs=[pl.BlockSpec(memory_space=pl.ANY)] * 2,
        out_specs=pl.BlockSpec(memory_space=pltpu.VMEM),
        scratch_shapes=[
            pltpu.VMEM((SERIES_ROWS, 1, 128), jnp.float32),
            pltpu.VMEM((1, LEAD * GROUP_COLS), jnp.float32),
            pltpu.VMEM((GROUPS, SLOT_ROWS, 1, 128), jnp.float32),
            pltpu.VMEM((2, 4, SLOT_ROWS, 128), jnp.float32),
            pltpu.VMEM((WIN_DEV, 128, TILE), jnp.bfloat16),
            pltpu.VMEM((WIN_DEV, 128, TILE), jnp.bfloat16),
            pltpu.VMEM((TILE, 128), jnp.bfloat16),
            pltpu.VMEM((WIN_DEV, TILE, 128), jnp.float32),
            pltpu.VMEM((WIN_DEV, 8, TILE), jnp.float32),
            pltpu.VMEM((WIN_DEV, 8, TILE), jnp.float32),
            pltpu.VMEM((2, WIN_DEV, TILE), jnp.float32),
            pltpu.VMEM((2, WIN_DEV, TILE), jnp.float32),
            pltpu.SemaphoreType.DMA((2,)),
            pltpu.SemaphoreType.DMA((GROUPS,)),
            pltpu.SemaphoreType.DMA((GROUPS,)),
            pltpu.SemaphoreType.DMA((8, WIN_DEV)),
            pltpu.SemaphoreType.DMA((8, WIN_DEV)),
            pltpu.SemaphoreType.DMA((2,)),
            pltpu.SemaphoreType.DMA((2,)),
        ],
        compiler_params=pltpu.CompilerParams(collective_id=0, has_side_effects=True, vmem_limit_bytes=56 * 2**20),
        name="connect",
    )(tick_bars.reshape(TICK_ROWS, 1, 128), prior_bars.reshape(1, LEAD * GROUP_COLS))
    return sums[0] + sums[1]


def solution(mesh):
    in_specs = (P("asset", "tm", None), P("asset", "tm", None))
    out_specs = P("tm", "asset")
    return jax.shard_map(shards, mesh=mesh, in_specs=in_specs, out_specs=out_specs, check_vma=False)
```

time: 62 us -> 56 us (0.903)
  Pallas kernels: 59 us -> 54.4 us
  local copies, waits for them, and re-layouts: 2.79 us -> 0 us
  other arithmetic: 0 us -> 1.52 us
    pallas_call x1, Pallas kernels: 59 us -> 54.4 us  [shards(): pl.pallas_call(kernel, out_shape=jax.ShapeDtypeStruct((2, WIN_DEV, TILE),...]
    add x0 -> x1, other arithmetic: none -> 1.52 us  [shards(): return sums[0] + sums[1]]
    unnamed x1 -> x0, local copies, waits for them, and re-layouts: 1.48 us -> none
    pad x1 -> x0, local copies, waits for them, and re-layouts: 1.31 us -> none  [shards(): jnp.pad(prior_bars.reshape(1, -1), ((0, 0), (0, LEAD_ROWS * 128 - LEAD *...]
where the time goes in v3:
time: 56 us; the launch traced here: 55.9 us
  Pallas kernels  54.4 us (97%)
  other arithmetic  1.52 us (3%)
    pallas_call x1, Pallas kernels, shards(): pl.pallas_call(kernel, out_shape=jax.ShapeDtypeStruct((2, WIN_DEV, TILE),...  54.4 us
    add x1, other arithmetic, shards(): return sums[0] + sums[1]  1.52 us

profile of v3, /device:TPU:1, one launch (start us, length us, event | category | flops | bytes accessed | tf_op | source)
XLA Modules:
  0.0 55.9 jit_solution(1768791538968521024)
XLA Ops:
  0.0 54.4 %connect.1 = f32[2,3,4096]{2,1,0:T(4,128)} custom-call(f32[480,1,128]{2,1,0:T(1,128)} %bitcast.4, f32[1,1600]{1,0:T(1,128)} %bitcast.5), custom_call_target="tpu_custom_call" | custom-call | tf_op jit(solution)/shard_map/connect/pallas_call | solution.py:330
  54.4 1.5 %add_bitcast_fusion = f32[3,4096]{1,0:T(4,128)} fusion(f32[2,3,4096]{2,1,0:T(4,128)} %connect.1), kind=kLoop, calls=%fused_computation | loop fusion | flops 12288 | bytes 147456 | tf_op jit(solution)/shard_map/add | solution.py:359

commit v4 on v3

--- a/solution.py
+++ b/solution.py
@@ -46,7 +46,7 @@
     return jnp.sum(a.reshape(a.shape[0] // 8, 8, a.shape[1]), axis=0)
 
 
-def prepare(raw_ref, bars, scaled, lhs_ref, chunk, half):
+def prepare(raw_ref, bars, ready, turned, chunk, half):
     low = lax.broadcasted_iota(jnp.int32, (SLOT_ROWS, 128), 1) < GROUP_COLS
     valid = lax.broadcasted_iota(jnp.int32, (16, 128), 0) < SPAN // 2
     aligned = half == 1
@@ -58,7 +58,7 @@
         bars[0, p] = jnp.where(aligned, even, odd)
         bars[1, p] = jnp.where(aligned, odd, pltpu.roll(even, SLOT_ROWS - 1, 0))
     for p in range(4):
-        at = pl.ds(pl.multiple_of(chunk * 512 + p * 128, 128), 128)
+        at = pl.ds(p * 128, 128)
         parts = []
         for w in range(WIN_DEV):
             first = w * STRIDE
@@ -70,15 +70,22 @@
             squares = jnp.sum(even * even + odd * odd, axis=0, keepdims=True)
             scale = lax.rsqrt(jnp.maximum(squares, FLOOR_SQUARES))
             even, odd = (even * scale).astype(jnp.bfloat16), (odd * scale).astype(jnp.bfloat16)
-            scaled[w, pl.ds(32 * w, 16), at] = even
-            scaled[w, pl.ds(32 * w + 16, 16), at] = odd
+            ready[w, pl.ds(0, 16), at] = even
+            ready[w, pl.ds(16, 16), at] = odd
             parts += [even, odd]
         parts.append(jnp.zeros((32, 128), jnp.bfloat16))
-        lhs_ref[at, :] = jnp.concatenate(parts, axis=0).T
+        turned[at, :] = jnp.concatenate(parts, axis=0).T
+
+
+def settle(ready, turned, scaled, lhs_ref, chunk):
+    at = pl.ds(pl.multiple_of(chunk * 512, 512), 512)
+    for w in range(WIN_DEV):
+        scaled[w, pl.ds(32 * w, 32), at] = ready[w]
+    lhs_ref[at, :] = turned[...]
 
 
 def kernel(
-    tick_ref, prior_ref, out_ref, series, prior, own_raw, bars, own, other, lhs_ref, rows, own_cols, other_cols, result, arrived,
+    tick_ref, prior_ref, out_ref, series, prior, own_raw, bars, ready, turned, own, other, lhs_ref, rows, own_cols, other_cols, result, arrived,
     load_sem, send_sem, own_sem, pass_sem, other_sem, result_send, result_recv,
 ):
     pair, core, half = place()
@@ -173,14 +180,20 @@
         for w in range(WIN_DEV):
             passing(q, w).start()
 
+    def chunk_of(q):
+        return lax.bitwise_xor(me // 8, q)
+
     def receive(q):
-        chunk = lax.bitwise_xor(me // 8, q)
         for j in range(8):
-            g = chunk * 8 + j
+            g = chunk_of(q) * 8 + j
             ref = own_raw.at[g, pl.ds(0, MSG_ROWS)]
             pltpu.make_async_copy(ref, ref, own_sem.at[g]).wait()
-        prepare(own_raw, bars, own, lhs_ref, chunk, half)
-        return chunk
+
+    def prepare_chunk(q):
+        prepare(own_raw, bars, ready, turned, chunk_of(q), half)
+
+    def settle_chunk(q):
+        settle(ready, turned, own, lhs_ref, chunk_of(q))
 
     def block(i):
         return pl.ds(pl.multiple_of(i * BLOCK, BLOCK), BLOCK)
@@ -191,44 +204,52 @@
             cols[w, :, col_at] += fold_rows(a)
         return a[:, :128] + a[:, 128:]
 
-    def early(q, carry):
-        chunk = receive(q)
-
-        def with_earlier(r, carry):
-            left = lax.bitwise_xor(me // 8, r)
-            for w in range(WIN_DEV):
-                for i in range(2):
-                    row_at = block(2 * chunk + i)
-                    rows[w, row_at, :] += pairs(w, row_at, block(2 * left), own, own_cols) + pairs(
-                        w, row_at, block(2 * left + 1), own, own_cols
-                    )
-            return carry
-
+    for q in range(4):
+        receive(q)
+        prepare_chunk(q)
+        settle_chunk(q)
+        chunk = chunk_of(q)
         first, second = block(2 * chunk), block(2 * chunk + 1)
         for w in range(WIN_DEV):
-            rows[w, first, :] += pairs(w, first, first, own, None) + pairs(w, first, second, own, own_cols)
-            rows[w, second, :] += pairs(w, second, second, own, None)
+            one = pairs(w, first, first, own, None) + pairs(w, first, second, own, own_cols)
+            two = pairs(w, second, second, own, None)
+            for r in range(q):
+                for d in range(2):
+                    col_at = block(2 * chunk_of(r) + d)
+                    one = one + pairs(w, first, col_at, own, own_cols)
+                    two = two + pairs(w, second, col_at, own, own_cols)
+            rows[w, first, :] += one
+            rows[w, second, :] += two
         pass_on(q)
-        lax.fori_loop(0, q, with_earlier, 0)
-        return carry
-
-    lax.fori_loop(0, 4, early, 0)
     first_half = me // 32
     near, far = first_half * 8, 8 - first_half * 8
 
+    def with_near(q, w, i):
+        row_at = block(2 * chunk_of(q) + i)
+        total = rows[w, row_at, :]
+        for d in range(8):
+            total = total + pairs(w, row_at, block(near + d), own, own_cols)
+        rows[w, row_at, :] = total
+
     def late(q, carry):
-        chunk = receive(q)
+        settle_chunk(q)
+        receive(q + 1)
         for i in range(2):
-            row_at = block(2 * chunk + i)
             for w in range(WIN_DEV):
-                total = rows[w, row_at, :]
-                for d in range(8):
-                    total = total + pairs(w, row_at, block(near + d), own, own_cols)
-                rows[w, row_at, :] = total
+                with_near(q, w, i)
+            if i == 0:
+                prepare_chunk(q + 1)
         pass_on(q)
         return carry
 
-    lax.fori_loop(4, 8, late, 0)
+    receive(4)
+    prepare_chunk(4)
+    lax.fori_loop(4, 7, late, 0)
+    settle_chunk(7)
+    pass_on(7)
+    for i in range(2):
+        for w in range(WIN_DEV):
+            with_near(7, w, i)
 
     def receive_other(q, carry):
         for w in range(WIN_DEV):
@@ -260,42 +281,63 @@
 
     lax.fori_loop(0, 2, across_tiles, 0)
 
-    for i in range(8):
-        row_at = block(far + i)
-        low = i % 4
-        half_at = pl.ds(pl.multiple_of((far + low) * BLOCK + (i // 4) * 128, 128), 128)
-        for w in range(WIN_DEV):
-            total = rows[w, row_at, :]
-            for d in range(4):
-                total = total + pairs(w, row_at, block(far + (i + d) % 8), own, own_cols if d else None)
-            rows[w, row_at, :] = total
-            rows[w, half_at, :] += pairs(w, half_at, block(far + low + 4), own, own_cols)
-            if i >= 4:
-                sum_rows(w, far + low, rows[w, block(far + low), :])
-                sum_rows(w, far + i, rows[w, row_at, :])
-
-    scale = math.sqrt(SPAN) / ASSETS
-    for w in range(WIN_DEV):
-        one = pl.ds(w, 1)
-        result[1, one, :] = jnp.sum(other_cols[w], axis=0, keepdims=True) * scale
-        result[0, one, :] = (result[0, one, :] + jnp.sum(own_cols[w], axis=0, keepdims=True)) * scale
-
-    def result_copy(which):
-        tile = core if which == 0 else 1 - core
+    def result_copy(tile, part, which):
+        at = pl.ds(pl.multiple_of(part * HALF, HALF), HALF)
         return pltpu.make_async_remote_copy(
-            src_ref=result.at[which],
-            dst_ref=arrived.at[which],
-            send_sem=result_send.at[which],
-            recv_sem=result_recv.at[which],
+            src_ref=result.at[which, :, at],
+            dst_ref=arrived.at[which, :, at],
+            send_sem=result_send.at[which, part],
+            recv_sem=result_recv.at[which, part],
             device_id=(pair * 2 + half, tile),
             device_id_type=MESH,
         )
 
-    result_copy(1).start()
-
-    @pl.when(core != half)
-    def _():
-        result_copy(0).start()
+    scale = math.sqrt(SPAN) / ASSETS
+
+    def sum_columns(part):
+        at = pl.ds(pl.multiple_of(part * HALF, HALF), HALF)
+        for w in range(WIN_DEV):
+            one = pl.ds(w, 1)
+            result[0, one, at] = (result[0, one, at] + jnp.sum(own_cols[w, :, at], axis=0, keepdims=True)) * scale
+
+    def send_main(part):
+        @pl.when(core != half)
+        def _():
+            result_copy(core, part, 0).start()
+
+    for w in range(WIN_DEV):
+        result[1, pl.ds(w, 1), :] = jnp.sum(other_cols[w], axis=0, keepdims=True) * scale
+    sum_columns(first_half)
+
+    def square(h, carry):
+        for i in range(4):
+            at_block = far + 4 * h + i
+            row_at = block(at_block)
+            half_at = pl.ds(pl.multiple_of((far + i) * BLOCK + h * 128, 128), 128)
+            for w in range(WIN_DEV):
+                total = rows[w, row_at, :]
+                for d in range(4):
+                    col = far + lax.rem(4 * h + i + d, 8)
+                    total = total + pairs(w, row_at, block(col), own, own_cols if d else None)
+                rows[w, row_at, :] = total
+                rows[w, half_at, :] += pairs(w, half_at, block(far + i + 4), own, own_cols)
+                sum_rows(w, far + i, rows[w, block(far + i), :])
+                sum_rows(w, at_block, rows[w, row_at, :])
+
+        @pl.when(h == 0)
+        def _():
+            result_copy(1 - core, 0, 1).start()
+            result_copy(1 - core, 1, 1).start()
+            send_main(first_half)
+
+        return carry
+
+    lax.fori_loop(0, 2, square, 0)
+    sum_columns(1 - first_half)
+    for part in range(2):
+        result_copy(1 - core, part, 1).wait()
+    out_ref[1] = arrived[1]
+    send_main(1 - first_half)
 
     def finish_send(k, carry):
         remote(k).wait_send()
@@ -313,12 +355,13 @@
         return carry
 
     lax.fori_loop(0, 8, finish_pass, 0)
-    result_copy(1).wait()
-    out_ref[1] = arrived[1]
-
     @pl.when(core != half)
     def _():
-        result_copy(0).wait()
+        for part in range(2):
+            result_copy(core, part, 0).wait()
+
+    @pl.when(core != half)
+    def _():
         out_ref[0] = arrived[0]
 
     @pl.when(core == half)
@@ -337,6 +380,8 @@
             pltpu.VMEM((1, LEAD * GROUP_COLS), jnp.float32),
             pltpu.VMEM((GROUPS, SLOT_ROWS, 1, 128), jnp.float32),
             pltpu.VMEM((2, 4, SLOT_ROWS, 128), jnp.float32),
+            pltpu.VMEM((WIN_DEV, 32, 512), jnp.bfloat16),
+            pltpu.VMEM((512, 128), jnp.bfloat16),
             pltpu.VMEM((WIN_DEV, 128, TILE), jnp.bfloat16),
             pltpu.VMEM((WIN_DEV, 128, TILE), jnp.bfloat16),
             pltpu.VMEM((TILE, 128), jnp.bfloat16),
@@ -350,8 +395,8 @@
             pltpu.SemaphoreType.DMA((GROUPS,)),
             pltpu.SemaphoreType.DMA((8, WIN_DEV)),
             pltpu.SemaphoreType.DMA((8, WIN_DEV)),
-            pltpu.SemaphoreType.DMA((2,)),
-            pltpu.SemaphoreType.DMA((2,)),
+            pltpu.SemaphoreType.DMA((2, 2)),
+            pltpu.SemaphoreType.DMA((2, 2)),
         ],
         compiler_params=pltpu.CompilerParams(collective_id=0, has_side_effects=True, vmem_limit_bytes=56 * 2**20),
         name="connect",

time: 56 us -> 59.7 us (1.066)
  Pallas kernels: 54.4 us -> 58 us
    pallas_call x1, Pallas kernels: 54.4 us -> 58 us  [shards(): pl.pallas_call(kernel, out_shape=jax.ShapeDtypeStruct((2, WIN_DEV, TILE),...]
where the time goes in v4:
time: 59.7 us; the launch traced here: 59.5 us
  Pallas kernels  58 us (97%)
  other arithmetic  1.52 us (3%)
    pallas_call x1, Pallas kernels, shards(): pl.pallas_call(kernel, out_shape=jax.ShapeDtypeStruct((2, WIN_DEV, TILE),...  58 us
    add x1, other arithmetic, shards(): return sums[0] + sums[1]  1.52 us

profile of v4, /device:TPU:1, one launch (start us, length us, event | category | flops | bytes accessed | tf_op | source)
XLA Modules:
  0.0 59.5 jit_solution(12943947598539548181)
XLA Ops:
  0.0 58.0 %connect.1 = f32[2,3,4096]{2,1,0:T(4,128)} custom-call(f32[480,1,128]{2,1,0:T(1,128)} %bitcast.4, f32[1,1600]{1,0:T(1,128)} %bitcast.5), custom_call_target="tpu_custom_call" | custom-call | tf_op jit(solution)/shard_map/connect/pallas_call | solution.py:373
  58.0 1.5 %add_bitcast_fusion = f32[3,4096]{1,0:T(4,128)} fusion(f32[2,3,4096]{2,1,0:T(4,128)} %connect.1), kind=kLoop, calls=%fused_computation | loop fusion | flops 12288 | bytes 147456 | tf_op jit(solution)/shard_map/add | solution.py:404

commit v5 on v4

--- a/solution.py
+++ b/solution.py
@@ -27,8 +27,6 @@
 SLOT_ROWS = 24
 BLOCK = 256
 HALF = TILE // 2
-EXT = TILE + HALF
-UNROLL = 4
 
 
 def place():
@@ -85,7 +83,7 @@
 
 
 def kernel(
-    tick_ref, prior_ref, out_ref, series, prior, own_raw, bars, ready, turned, own, other, lhs_ref, rows, own_cols, other_cols, result, arrived,
+    tick_ref, prior_ref, out_ref, series, prior, own_raw, bars, ready, turned, own, other, lhs_ref, rows, own_cols, other_cols, line, far_sums, near_sums, arrived,
     load_sem, send_sem, own_sem, pass_sem, other_sem, result_send, result_recv,
 ):
     pair, core, half = place()
@@ -99,16 +97,19 @@
     barrier = pltpu.get_barrier_semaphore()
 
     def greet(j, carry):
-        g = lax.bitwise_xor(me, GROUPS - 1 - j)
-
-        @pl.when(jnp.logical_or(g != me, core != half))
-        def _():
-            pl.semaphore_signal(barrier, inc=1, device_id=(g, core), device_id_type=MESH)
-
-        return carry
-
-    lax.fori_loop(0, GROUPS, greet, 0)
+        k = GROUPS - 1 - j
+        target = 2 * lax.bitwise_xor(pair, lax.rem(k, 32)) + core
+        pl.semaphore_signal(
+            barrier, inc=1, device_id=(target, lax.bitwise_xor(half, k // 32)), device_id_type=MESH
+        )
+        return carry
+
+    lax.fori_loop(0, GROUPS - 1, greet, 0)
     pl.semaphore_signal(barrier, inc=1, device_id=(sibling, half), device_id_type=MESH)
+
+    @pl.when(core != half)
+    def _():
+        pl.semaphore_signal(barrier, inc=1, device_id=(sibling, core), device_id_type=MESH)
 
     prior_load.wait()
     low = lax.broadcasted_iota(jnp.int32, (1, 128), 1) < GROUP_COLS
@@ -133,9 +134,11 @@
     pl.semaphore_wait(barrier, GROUPS + jnp.where(core == half, 0, 1))
     load.wait()
 
+    my_slot = half * 32 + pair
+
     def message(k):
-        target_pair = lax.bitwise_xor(pair, k // 2)
-        target_half = lax.bitwise_xor(half, lax.rem(k, 2))
+        target_pair = lax.bitwise_xor(pair, lax.rem(k, 32))
+        target_half = lax.bitwise_xor(half, k // 32)
         start = (BLOCK_BARS * (2 * target_pair + target_half) + 1) // 2
         return target_pair, target_half, series.at[pl.ds(start, MSG_ROWS)]
 
@@ -143,30 +146,26 @@
         target_pair, target_half, src = message(k)
         return pltpu.make_async_remote_copy(
             src_ref=src,
-            dst_ref=own_raw.at[me, pl.ds(0, MSG_ROWS)],
-            send_sem=send_sem.at[k],
-            recv_sem=own_sem.at[me],
-            device_id=(target_pair * 2 + half, target_half),
+            dst_ref=own_raw.at[my_slot, pl.ds(0, MSG_ROWS)],
+            send_sem=send_sem,
+            recv_sem=own_sem.at[my_slot // 8],
+            device_id=(target_pair * 2 + core, target_half),
             device_id_type=MESH,
         )
 
-    @pl.when(core == half)
-    def _():
-        _, _, src = message(0)
-        pltpu.make_async_copy(src, own_raw.at[me, pl.ds(0, MSG_ROWS)], own_sem.at[me]).start()
-
-    @pl.when(core != half)
-    def _():
-        remote(0).start()
-
     def send(k, carry):
         remote(k).start()
         return carry
 
     lax.fori_loop(1, GROUPS, send, 0)
+    _, _, kept = message(0)
+    pltpu.make_async_copy(kept, own_raw.at[my_slot, pl.ds(0, MSG_ROWS)], own_sem.at[my_slot // 8]).start()
+
+    def chunk_of(q):
+        return lax.bitwise_xor(my_slot // 8, q)
 
     def passing(q, w):
-        at = pl.ds(pl.multiple_of(lax.bitwise_xor(me // 8, q) * 512, 512), 512)
+        at = pl.ds(pl.multiple_of(chunk_of(q) * 512, 512), 512)
         return pltpu.make_async_remote_copy(
             src_ref=own.at[w, pl.ds(32 * w, 32), at],
             dst_ref=other.at[w, pl.ds(32 * w, 32), at],
@@ -180,14 +179,9 @@
         for w in range(WIN_DEV):
             passing(q, w).start()
 
-    def chunk_of(q):
-        return lax.bitwise_xor(me // 8, q)
-
     def receive(q):
-        for j in range(8):
-            g = chunk_of(q) * 8 + j
-            ref = own_raw.at[g, pl.ds(0, MSG_ROWS)]
-            pltpu.make_async_copy(ref, ref, own_sem.at[g]).wait()
+        ref = own_raw.at[pl.ds(chunk_of(q) * 8, 8), pl.ds(0, MSG_ROWS)]
+        pltpu.make_async_copy(ref, ref, own_sem.at[chunk_of(q)]).wait()
 
     def prepare_chunk(q):
         prepare(own_raw, bars, ready, turned, chunk_of(q), half)
@@ -221,8 +215,7 @@
             rows[w, first, :] += one
             rows[w, second, :] += two
         pass_on(q)
-    first_half = me // 32
-    near, far = first_half * 8, 8 - first_half * 8
+    near, far = half * 8, 8 - half * 8
 
     def with_near(q, w, i):
         row_at = block(2 * chunk_of(q) + i)
@@ -233,13 +226,13 @@
 
     def late(q, carry):
         settle_chunk(q)
+        for w in range(WIN_DEV):
+            with_near(q, w, 0)
+        pass_on(q)
         receive(q + 1)
-        for i in range(2):
-            for w in range(WIN_DEV):
-                with_near(q, w, i)
-            if i == 0:
-                prepare_chunk(q + 1)
-        pass_on(q)
+        prepare_chunk(q + 1)
+        for w in range(WIN_DEV):
+            with_near(q, w, 1)
         return carry
 
     receive(4)
@@ -251,68 +244,9 @@
         for w in range(WIN_DEV):
             with_near(7, w, i)
 
-    def receive_other(q, carry):
-        for w in range(WIN_DEV):
-            passing(q, w).wait_recv()
-        return carry
-
-    def sum_rows(w, i, total):
-        for q in range(0, BLOCK, 128):
-            at = pl.ds(pl.multiple_of(i * BLOCK + q, 128), 128)
-            result[0, pl.ds(w, 1), at] = jnp.sum(total[q : q + 128].T, axis=0, keepdims=True)
-
-    def across_tiles(h, carry):
-        lax.fori_loop(4 * h, 4 * h + 4, receive_other, 0)
-        col_half = lax.bitwise_xor(first_half, h)
-        row_half = lax.rem(col_half + core, 2)
-
-        def step(i, carry):
-            row_at = block(row_half * 8 + i)
-            for w in range(WIN_DEV):
-                total = rows[w, row_at, :]
-                for d in range(8):
-                    total = total + pairs(w, row_at, block(col_half * 8 + d), other, other_cols)
-                rows[w, row_at, :] = total
-                sum_rows(w, row_half * 8 + i, total)
-            return carry
-
-        lax.fori_loop(0, 8, step, 0, unroll=UNROLL)
-        return carry
-
-    lax.fori_loop(0, 2, across_tiles, 0)
-
-    def result_copy(tile, part, which):
-        at = pl.ds(pl.multiple_of(part * HALF, HALF), HALF)
-        return pltpu.make_async_remote_copy(
-            src_ref=result.at[which, :, at],
-            dst_ref=arrived.at[which, :, at],
-            send_sem=result_send.at[which, part],
-            recv_sem=result_recv.at[which, part],
-            device_id=(pair * 2 + half, tile),
-            device_id_type=MESH,
-        )
-
-    scale = math.sqrt(SPAN) / ASSETS
-
-    def sum_columns(part):
-        at = pl.ds(pl.multiple_of(part * HALF, HALF), HALF)
-        for w in range(WIN_DEV):
-            one = pl.ds(w, 1)
-            result[0, one, at] = (result[0, one, at] + jnp.sum(own_cols[w, :, at], axis=0, keepdims=True)) * scale
-
-    def send_main(part):
-        @pl.when(core != half)
-        def _():
-            result_copy(core, part, 0).start()
-
-    for w in range(WIN_DEV):
-        result[1, pl.ds(w, 1), :] = jnp.sum(other_cols[w], axis=0, keepdims=True) * scale
-    sum_columns(first_half)
-
     def square(h, carry):
         for i in range(4):
-            at_block = far + 4 * h + i
-            row_at = block(at_block)
+            row_at = block(far + 4 * h + i)
             half_at = pl.ds(pl.multiple_of((far + i) * BLOCK + h * 128, 128), 128)
             for w in range(WIN_DEV):
                 total = rows[w, row_at, :]
@@ -321,58 +255,110 @@
                     total = total + pairs(w, row_at, block(col), own, own_cols if d else None)
                 rows[w, row_at, :] = total
                 rows[w, half_at, :] += pairs(w, half_at, block(far + i + 4), own, own_cols)
-                sum_rows(w, far + i, rows[w, block(far + i), :])
-                sum_rows(w, at_block, rows[w, row_at, :])
-
-        @pl.when(h == 0)
+        return carry
+
+    lax.fori_loop(0, 2, square, 0)
+
+    def finish_pass(q, carry):
+        for w in range(WIN_DEV):
+            passing(q, w).wait_send()
+        return carry
+
+    def receive_other(q, carry):
+        for w in range(WIN_DEV):
+            passing(q, w).wait_recv()
+        return carry
+
+    lax.fori_loop(0, 8, receive_other, 0)
+
+    scale = math.sqrt(SPAN) / ASSETS
+
+    def gather_sums(first_block, sums):
+        at = pl.ds(pl.multiple_of(first_block * BLOCK, BLOCK), HALF)
+        for w in range(WIN_DEV):
+            one = pl.ds(w, 1)
+            sums[core, one, :] = (line[one, at] + jnp.sum(own_cols[w, :, at], axis=0, keepdims=True)) * scale
+            sums[1 - core, one, :] = jnp.sum(other_cols[w, :, at], axis=0, keepdims=True) * scale
+
+    far_copy = pltpu.make_async_remote_copy(
+        src_ref=far_sums,
+        dst_ref=arrived.at[core],
+        send_sem=result_send.at[0],
+        recv_sem=result_recv.at[core],
+        device_id=(pair * 2 + half, 1 - half),
+        device_id_type=MESH,
+    )
+    near_copy = pltpu.make_async_remote_copy(
+        src_ref=near_sums,
+        dst_ref=arrived.at[core],
+        send_sem=result_send.at[1],
+        recv_sem=result_recv.at[core],
+        device_id=(sibling, half),
+        device_id_type=MESH,
+    )
+
+    def across(part, carry):
+        row_first = jnp.where(lax.rem(part, 2) == 0, far, near)
+        col_first = jnp.where(part < 2, far, near)
+        for t in range(2):
+            cols_from = col_first + 4 * lax.rem(t + core, 2)
+            for i in range(4):
+                at_block = row_first + 4 * t + i
+                row_at = block(at_block)
+                for w in range(WIN_DEV):
+                    total = rows[w, row_at, :]
+                    for d in range(4):
+                        total = total + pairs(w, row_at, block(cols_from + d), other, other_cols)
+                    rows[w, row_at, :] = total
+                    for p in range(0, BLOCK, 128):
+                        at = pl.ds(pl.multiple_of(at_block * BLOCK + p, 128), 128)
+                        line[pl.ds(w, 1), at] = jnp.sum(total[p : p + 128].T, axis=0, keepdims=True)
+
+        @pl.when(part == 2)
         def _():
-            result_copy(1 - core, 0, 1).start()
-            result_copy(1 - core, 1, 1).start()
-            send_main(first_half)
-
-        return carry
-
-    lax.fori_loop(0, 2, square, 0)
-    sum_columns(1 - first_half)
-    for part in range(2):
-        result_copy(1 - core, part, 1).wait()
-    out_ref[1] = arrived[1]
-    send_main(1 - first_half)
-
-    def finish_send(k, carry):
-        remote(k).wait_send()
-        return carry
+            gather_sums(far, far_sums)
+
+            sent = own_raw.at[pl.ds(0, GROUPS - 1), pl.ds(0, MSG_ROWS)]
+            pltpu.make_async_copy(sent, sent, send_sem).wait()
+            lax.fori_loop(0, 8, finish_pass, 0)
+            far_copy.start()
+
+        return carry
+
+    lax.fori_loop(0, 4, across, 0)
+    gather_sums(near, near_sums)
+
+    lanes_low = lax.broadcasted_iota(jnp.int32, (WIN_DEV, 128), 1) < GROUP_COLS
+
+    def write_out(first, second):
+        for p in range(HALF // 128):
+            at = pl.ds(p * 128, 128)
+            zero = first[0, :, at] + second[0, :, at]
+            one = first[1, :, at] + second[1, :, at]
+            out_ref[:, pl.ds(2 * p * 128, 128)] = jnp.where(lanes_low, zero, pltpu.roll(one, GROUP_COLS, 1))
+            out_ref[:, pl.ds((2 * p + 1) * 128, 128)] = jnp.where(lanes_low, pltpu.roll(zero, GROUP_COLS, 1), one)
 
     @pl.when(core != half)
     def _():
-        remote(0).wait_send()
-
-    lax.fori_loop(1, GROUPS, finish_send, 0)
-
-    def finish_pass(q, carry):
-        for w in range(WIN_DEV):
-            passing(q, w).wait_send()
-        return carry
-
-    lax.fori_loop(0, 8, finish_pass, 0)
-    @pl.when(core != half)
-    def _():
-        for part in range(2):
-            result_copy(core, part, 0).wait()
-
-    @pl.when(core != half)
-    def _():
-        out_ref[0] = arrived[0]
+        near_copy.start()
+        for d in range(2):
+            pltpu.make_async_copy(arrived.at[d], arrived.at[d], result_recv.at[d]).wait()
+        write_out(arrived.at[0], arrived.at[1])
+        near_copy.wait_send()
 
     @pl.when(core == half)
     def _():
-        out_ref[0] = result[0]
+        other_core = 1 - core
+        pltpu.make_async_copy(arrived.at[other_core], arrived.at[other_core], result_recv.at[other_core]).wait()
+        write_out(near_sums, arrived.at[other_core])
+
+    far_copy.wait_send()
 
 
 def shards(tick_bars, prior_bars):
-    sums = pl.pallas_call(
+    return pl.pallas_call(
         kernel,
-        out_shape=jax.ShapeDtypeStruct((2, WIN_DEV, TILE), jnp.float32),
+        out_shape=jax.ShapeDtypeStruct((WIN_DEV, TILE), jnp.float32),
         in_specs=[pl.BlockSpec(memory_space=pl.ANY)] * 2,
         out_specs=pl.BlockSpec(memory_space=pltpu.VMEM),
         scratch_shapes=[
@@ -388,20 +374,21 @@
             pltpu.VMEM((WIN_DEV, TILE, 128), jnp.float32),
             pltpu.VMEM((WIN_DEV, 8, TILE), jnp.float32),
             pltpu.VMEM((WIN_DEV, 8, TILE), jnp.float32),
-            pltpu.VMEM((2, WIN_DEV, TILE), jnp.float32),
-            pltpu.VMEM((2, WIN_DEV, TILE), jnp.float32),
+            pltpu.VMEM((WIN_DEV, TILE), jnp.float32),
+            pltpu.VMEM((2, WIN_DEV, HALF), jnp.float32),
+            pltpu.VMEM((2, WIN_DEV, HALF), jnp.float32),
+            pltpu.VMEM((2, 2, WIN_DEV, HALF), jnp.float32),
             pltpu.SemaphoreType.DMA((2,)),
-            pltpu.SemaphoreType.DMA((GROUPS,)),
-            pltpu.SemaphoreType.DMA((GROUPS,)),
+            pltpu.SemaphoreType.DMA,
+            pltpu.SemaphoreType.DMA((8,)),
             pltpu.SemaphoreType.DMA((8, WIN_DEV)),
             pltpu.SemaphoreType.DMA((8, WIN_DEV)),
-            pltpu.SemaphoreType.DMA((2, 2)),
-            pltpu.SemaphoreType.DMA((2, 2)),
+            pltpu.SemaphoreType.DMA((2,)),
+            pltpu.SemaphoreType.DMA((2,)),
         ],
         compiler_params=pltpu.CompilerParams(collective_id=0, has_side_effects=True, vmem_limit_bytes=56 * 2**20),
         name="connect",
     )(tick_bars.reshape(TICK_ROWS, 1, 128), prior_bars.reshape(1, LEAD * GROUP_COLS))
-    return sums[0] + sums[1]
 
 
 def solution(mesh):

time: 59.7 us -> 53.2 us (0.89)
  Pallas kernels: 58 us -> 51.6 us
  other arithmetic: 1.52 us -> 0 us
  local copies, waits for them, and re-layouts: 0 us -> 1.48 us
    pallas_call x1, Pallas kernels: 58 us -> 51.6 us  [shards(): pl.pallas_call(kernel, out_shape=jax.ShapeDtypeStruct((WIN_DEV, TILE), jn...]
    add x1 -> x0, other arithmetic: 1.52 us -> none  [shards(): return sums[0] + sums[1]]
    unnamed x0 -> x1, local copies, waits for them, and re-layouts: none -> 1.48 us
where the time goes in v5:
time: 53.2 us; the launch traced here: 53.1 us
  Pallas kernels  51.6 us (97%)
  local copies, waits for them, and re-layouts  1.48 us (3%)
    pallas_call x1, Pallas kernels, shards(): pl.pallas_call(kernel, out_shape=jax.ShapeDtypeStruct((WIN_DEV, TILE), jn...  51.6 us
    unnamed x1, local copies, waits for them, and re-layouts  1.48 us

profile of v5, /device:TPU:1, one launch (start us, length us, event | category | flops | bytes accessed | tf_op | source)
XLA Modules:
  0.0 53.1 jit_solution(9772285928884639868)
XLA Ops:
  0.0 51.6 %connect.1 = f32[3,4096]{1,0:T(4,128)} custom-call(f32[480,1,128]{2,1,0:T(1,128)} %bitcast.2, f32[1,1600]{1,0:T(1,128)} %bitcast.3), custom_call_target="tpu_custom_call" | custom-call | tf_op jit(solution)/shard_map/connect/pallas_call | solution.py:359
  51.6 1.5 %copy.4 = f32[3,4096]{1,0:T(4,128)} copy(f32[3,4096]{1,0:T(4,128)} %connect.1) | data formatting | bytes 98304

commit v6 on v5

--- a/solution.py
+++ b/solution.py
@@ -20,11 +20,12 @@
 GROUPS = 64
 GROUP_COLS = TILE // GROUPS
 BLOCK_BARS = WIN_DEV * STRIDE
-LEAD_ROWS = 13
+FIRST_ROW = 3
+TICK_FIRST = 16
 TICK_ROWS = 480
-SERIES_ROWS = LEAD_ROWS + TICK_ROWS + 1
-MSG_ROWS = 21
-SLOT_ROWS = 24
+SERIES_ROWS = TICK_FIRST + TICK_ROWS + 8
+PIECES = 5
+FAR_AFTER = 0
 BLOCK = 256
 HALF = TILE // 2
 
@@ -44,17 +45,15 @@
     return jnp.sum(a.reshape(a.shape[0] // 8, 8, a.shape[1]), axis=0)
 
 
-def prepare(raw_ref, bars, ready, turned, chunk, half):
-    low = lax.broadcasted_iota(jnp.int32, (SLOT_ROWS, 128), 1) < GROUP_COLS
+def prepare(raw_ref, bars, ready, turned, chunk):
+    low = lax.broadcasted_iota(jnp.int32, (4, 128), 1) < GROUP_COLS
     valid = lax.broadcasted_iota(jnp.int32, (16, 128), 0) < SPAN // 2
-    aligned = half == 1
     for p in range(4):
         slot = chunk * 8 + 2 * p
-        a, b = raw_ref[slot, :, 0, :], raw_ref[slot + 1, :, 0, :]
-        even = jnp.where(low, a, pltpu.roll(b, GROUP_COLS, 1))
-        odd = jnp.where(low, pltpu.roll(a, GROUP_COLS, 1), b)
-        bars[0, p] = jnp.where(aligned, even, odd)
-        bars[1, p] = jnp.where(aligned, odd, pltpu.roll(even, SLOT_ROWS - 1, 0))
+        for j in range(PIECES):
+            a, b = raw_ref[slot, j], raw_ref[slot + 1, j]
+            bars[0, p, pl.ds(4 * j, 4), :] = jnp.where(low, a, pltpu.roll(b, GROUP_COLS, 1))
+            bars[1, p, pl.ds(4 * j, 4), :] = jnp.where(low, pltpu.roll(a, GROUP_COLS, 1), b)
     for p in range(4):
         at = pl.ds(p * 128, 128)
         parts = []
@@ -83,7 +82,7 @@
 
 
 def kernel(
-    tick_ref, prior_ref, out_ref, series, prior, own_raw, bars, ready, turned, own, other, lhs_ref, rows, own_cols, other_cols, line, far_sums, near_sums, arrived,
+    tick_ref, prior_ref, out_ref, series, prior, messages, own_raw, bars, ready, turned, own, other, lhs_ref, rows, own_cols, other_cols, line, far_sums, near_sums, arrived,
     load_sem, send_sem, own_sem, pass_sem, other_sem, result_send, result_recv,
 ):
     pair, core, half = place()
@@ -91,7 +90,7 @@
     sibling = pair * 2 + 1 - core
     prior_load = pltpu.make_async_copy(prior_ref, prior, load_sem.at[0])
     prior_load.start()
-    load = pltpu.make_async_copy(tick_ref, series.at[pl.ds(LEAD_ROWS, TICK_ROWS)], load_sem.at[1])
+    load = pltpu.make_async_copy(tick_ref, series.at[pl.ds(TICK_FIRST, TICK_ROWS)], load_sem.at[1])
     load.start()
 
     barrier = pltpu.get_barrier_semaphore()
@@ -113,10 +112,24 @@
 
     prior_load.wait()
     low = lax.broadcasted_iota(jnp.int32, (1, 128), 1) < GROUP_COLS
-    series[0] = jnp.where(low, 0.0, pltpu.roll(prior[:, 0:128], GROUP_COLS, 1))
-    for r in range(1, LEAD_ROWS):
-        series[r] = prior[:, 128 * r - GROUP_COLS : 128 * r + GROUP_COLS]
-    series[LEAD_ROWS + TICK_ROWS] = jnp.zeros((1, 128), jnp.float32)
+    series[pl.ds(FIRST_ROW, 1), :] = jnp.where(low, 0.0, pltpu.roll(prior[:, 0:128], GROUP_COLS, 1))
+    for r in range(1, TICK_FIRST - FIRST_ROW):
+        series[pl.ds(FIRST_ROW + r, 1), :] = prior[:, 128 * r - GROUP_COLS : 128 * r + GROUP_COLS]
+    series[pl.ds(TICK_FIRST + TICK_ROWS, 8), :] = jnp.zeros((8, 128), jnp.float32)
+    load.wait()
+
+    lows = lax.broadcasted_iota(jnp.int32, (4, 128), 1) < GROUP_COLS
+
+    def assemble(t, carry):
+        even = FIRST_ROW + BLOCK_BARS * t
+        odd = FIRST_ROW + BLOCK_BARS * t + 8
+        for j in range(PIECES):
+            here, after = series[pl.ds(even + 4 * j, 4), :], series[pl.ds(even + 4 * j + 1, 4), :]
+            messages[t, j] = pltpu.roll(jnp.where(lows, after, here), GROUP_COLS, 1)
+            messages[32 + t, j] = series[pl.ds(odd + 4 * j, 4), :]
+        return carry
+
+    lax.fori_loop(0, 32, assemble, 0, unroll=2)
     own_cols[...] = jnp.zeros_like(own_cols)
     other_cols[...] = jnp.zeros_like(other_cols)
 
@@ -132,21 +145,19 @@
 
     lax.fori_loop(0, TILE // 256, clear, 0)
     pl.semaphore_wait(barrier, GROUPS + jnp.where(core == half, 0, 1))
-    load.wait()
 
     my_slot = half * 32 + pair
 
     def message(k):
         target_pair = lax.bitwise_xor(pair, lax.rem(k, 32))
         target_half = lax.bitwise_xor(half, k // 32)
-        start = (BLOCK_BARS * (2 * target_pair + target_half) + 1) // 2
-        return target_pair, target_half, series.at[pl.ds(start, MSG_ROWS)]
+        return target_pair, target_half, messages.at[target_half * 32 + target_pair]
 
     def remote(k):
         target_pair, target_half, src = message(k)
         return pltpu.make_async_remote_copy(
             src_ref=src,
-            dst_ref=own_raw.at[my_slot, pl.ds(0, MSG_ROWS)],
+            dst_ref=own_raw.at[my_slot],
             send_sem=send_sem,
             recv_sem=own_sem.at[my_slot // 8],
             device_id=(target_pair * 2 + core, target_half),
@@ -157,9 +168,9 @@
         remote(k).start()
         return carry
 
-    lax.fori_loop(1, GROUPS, send, 0)
+    lax.fori_loop(1, 32, send, 0)
     _, _, kept = message(0)
-    pltpu.make_async_copy(kept, own_raw.at[my_slot, pl.ds(0, MSG_ROWS)], own_sem.at[my_slot // 8]).start()
+    pltpu.make_async_copy(kept, own_raw.at[my_slot], own_sem.at[my_slot // 8]).start()
 
     def chunk_of(q):
         return lax.bitwise_xor(my_slot // 8, q)
@@ -180,11 +191,11 @@
             passing(q, w).start()
 
     def receive(q):
-        ref = own_raw.at[pl.ds(chunk_of(q) * 8, 8), pl.ds(0, MSG_ROWS)]
+        ref = own_raw.at[pl.ds(chunk_of(q) * 8, 8)]
         pltpu.make_async_copy(ref, ref, own_sem.at[chunk_of(q)]).wait()
 
     def prepare_chunk(q):
-        prepare(own_raw, bars, ready, turned, chunk_of(q), half)
+        prepare(own_raw, bars, ready, turned, chunk_of(q))
 
     def settle_chunk(q):
         settle(ready, turned, own, lhs_ref, chunk_of(q))
@@ -198,8 +209,12 @@
             cols[w, :, col_at] += fold_rows(a)
         return a[:, :128] + a[:, 128:]
 
+    if FAR_AFTER < 0:
+        lax.fori_loop(32, GROUPS, send, 0)
     for q in range(4):
         receive(q)
+        if q == FAR_AFTER:
+            lax.fori_loop(32, GROUPS, send, 0)
         prepare_chunk(q)
         settle_chunk(q)
         chunk = chunk_of(q)
@@ -318,7 +333,7 @@
         def _():
             gather_sums(far, far_sums)
 
-            sent = own_raw.at[pl.ds(0, GROUPS - 1), pl.ds(0, MSG_ROWS)]
+            sent = own_raw.at[pl.ds(0, GROUPS - 1)]
             pltpu.make_async_copy(sent, sent, send_sem).wait()
             lax.fori_loop(0, 8, finish_pass, 0)
             far_copy.start()
@@ -362,10 +377,11 @@
         in_specs=[pl.BlockSpec(memory_space=pl.ANY)] * 2,
         out_specs=pl.BlockSpec(memory_space=pltpu.VMEM),
         scratch_shapes=[
-            pltpu.VMEM((SERIES_ROWS, 1, 128), jnp.float32),
+            pltpu.VMEM((SERIES_ROWS, 128), jnp.float32),
             pltpu.VMEM((1, LEAD * GROUP_COLS), jnp.float32),
-            pltpu.VMEM((GROUPS, SLOT_ROWS, 1, 128), jnp.float32),
-            pltpu.VMEM((2, 4, SLOT_ROWS, 128), jnp.float32),
+            pltpu.VMEM((GROUPS, PIECES, 4, 128), jnp.float32),
+            pltpu.VMEM((GROUPS, PIECES, 4, 128), jnp.float32),
+            pltpu.VMEM((2, 4, 24, 128), jnp.float32),
             pltpu.VMEM((WIN_DEV, 32, 512), jnp.bfloat16),
             pltpu.VMEM((512, 128), jnp.bfloat16),
             pltpu.VMEM((WIN_DEV, 128, TILE), jnp.bfloat16),
@@ -388,7 +404,7 @@
         ],
         compiler_params=pltpu.CompilerParams(collective_id=0, has_side_effects=True, vmem_limit_bytes=56 * 2**20),
         name="connect",
-    )(tick_bars.reshape(TICK_ROWS, 1, 128), prior_bars.reshape(1, LEAD * GROUP_COLS))
+    )(tick_bars.reshape(TICK_ROWS, 128), prior_bars.reshape(1, LEAD * GROUP_COLS))
 
 
 def solution(mesh):

time: 53.2 us -> 51.8 us (0.974)
  Pallas kernels: 51.6 us -> 50.2 us
    pallas_call x1, Pallas kernels: 51.6 us -> 50.2 us  [shards(): pl.pallas_call(kernel, out_shape=jax.ShapeDtypeStruct((WIN_DEV, TILE), jn...]
where the time goes in v6:
time: 51.8 us; the launch traced here: 51.7 us
  Pallas kernels  50.2 us (97%)
  local copies, waits for them, and re-layouts  1.48 us (3%)
    pallas_call x1, Pallas kernels, shards(): pl.pallas_call(kernel, out_shape=jax.ShapeDtypeStruct((WIN_DEV, TILE), jn...  50.2 us
    unnamed x1, local copies, waits for them, and re-layouts  1.48 us

profile of v6, /device:TPU:1, one launch (start us, length us, event | category | flops | bytes accessed | tf_op | source)
XLA Modules:
  0.0 51.7 jit_solution(7238987322517325206)
XLA Ops:
  0.0 50.2 %connect.1 = f32[3,4096]{1,0:T(4,128)} custom-call(f32[480,128]{1,0:T(8,128)} %bitcast.2, f32[1,1600]{1,0:T(1,128)} %bitcast.3), custom_call_target="tpu_custom_call" | custom-call | tf_op jit(solution)/shard_map/connect/pallas_call | solution.py:374
  50.2 1.5 %copy.4 = f32[3,4096]{1,0:T(4,128)} copy(f32[3,4096]{1,0:T(4,128)} %connect.1) | data formatting | bytes 98304

commit v7 on v6

--- a/solution.py
+++ b/solution.py
@@ -25,7 +25,6 @@
 TICK_ROWS = 480
 SERIES_ROWS = TICK_FIRST + TICK_ROWS + 8
 PIECES = 5
-FAR_AFTER = 0
 BLOCK = 256
 HALF = TILE // 2
 
@@ -83,7 +82,7 @@
 
 def kernel(
     tick_ref, prior_ref, out_ref, series, prior, messages, own_raw, bars, ready, turned, own, other, lhs_ref, rows, own_cols, other_cols, line, far_sums, near_sums, arrived,
-    load_sem, send_sem, own_sem, pass_sem, other_sem, result_send, result_recv,
+    load_sem, send_sem, own_sem, pass_sem, other_sem, result_send, result_recv, far_ready,
 ):
     pair, core, half = place()
     me = pair * 2 + core
@@ -96,15 +95,13 @@
     barrier = pltpu.get_barrier_semaphore()
 
     def greet(j, carry):
-        k = GROUPS - 1 - j
-        target = 2 * lax.bitwise_xor(pair, lax.rem(k, 32)) + core
-        pl.semaphore_signal(
-            barrier, inc=1, device_id=(target, lax.bitwise_xor(half, k // 32)), device_id_type=MESH
-        )
-        return carry
-
-    lax.fori_loop(0, GROUPS - 1, greet, 0)
+        target = 2 * lax.bitwise_xor(pair, 31 - j) + core
+        pl.semaphore_signal(barrier, inc=1, device_id=(target, half), device_id_type=MESH)
+        return carry
+
+    lax.fori_loop(0, 31, greet, 0)
     pl.semaphore_signal(barrier, inc=1, device_id=(sibling, half), device_id_type=MESH)
+    pl.semaphore_signal(barrier, inc=1, device_id=(me, 1 - half), device_id_type=MESH)
 
     @pl.when(core != half)
     def _():
@@ -120,31 +117,31 @@
 
     lows = lax.broadcasted_iota(jnp.int32, (4, 128), 1) < GROUP_COLS
 
-    def assemble(t, carry):
-        even = FIRST_ROW + BLOCK_BARS * t
-        odd = FIRST_ROW + BLOCK_BARS * t + 8
+    def shifted(t, carry):
+        row = FIRST_ROW + BLOCK_BARS * t
         for j in range(PIECES):
-            here, after = series[pl.ds(even + 4 * j, 4), :], series[pl.ds(even + 4 * j + 1, 4), :]
+            here, after = series[pl.ds(row + 4 * j, 4), :], series[pl.ds(row + 4 * j + 1, 4), :]
             messages[t, j] = pltpu.roll(jnp.where(lows, after, here), GROUP_COLS, 1)
-            messages[32 + t, j] = series[pl.ds(odd + 4 * j, 4), :]
-        return carry
-
-    lax.fori_loop(0, 32, assemble, 0, unroll=2)
-    own_cols[...] = jnp.zeros_like(own_cols)
-    other_cols[...] = jnp.zeros_like(other_cols)
-
-    def clear(i, carry):
-        at = pl.ds(pl.multiple_of(i * 256, 256), 256)
-        for w in range(WIN_DEV):
-            rows[w, at, :] = jnp.zeros((256, 128), jnp.float32)
-            for first, last in ((0, 32 * w), (32 * w + 32, 128)):
-                if last > first:
-                    own[w, pl.ds(first, last - first), at] = jnp.zeros((last - first, 256), jnp.bfloat16)
-                    other[w, pl.ds(first, last - first), at] = jnp.zeros((last - first, 256), jnp.bfloat16)
-        return carry
-
-    lax.fori_loop(0, TILE // 256, clear, 0)
-    pl.semaphore_wait(barrier, GROUPS + jnp.where(core == half, 0, 1))
+        return carry
+
+    def aligned(t, carry):
+        row = FIRST_ROW + BLOCK_BARS * t + 8
+        for j in range(PIECES):
+            messages[32 + t, j] = series[pl.ds(row + 4 * j, 4), :]
+        return carry
+
+    def assemble(target_half):
+        @pl.when(target_half == 0)
+        def _():
+            lax.fori_loop(0, 32, shifted, 0, unroll=4)
+
+        @pl.when(target_half == 1)
+        def _():
+            lax.fori_loop(0, 32, aligned, 0, unroll=4)
+
+    assemble(half)
+    pl.semaphore_wait(barrier, 33 + jnp.where(core == half, 0, 1))
+    pl.semaphore_signal(far_ready, inc=1, device_id=(me, 1 - half), device_id_type=MESH)
 
     my_slot = half * 32 + pair
 
@@ -172,6 +169,22 @@
     _, _, kept = message(0)
     pltpu.make_async_copy(kept, own_raw.at[my_slot], own_sem.at[my_slot // 8]).start()
 
+    assemble(1 - half)
+    own_cols[...] = jnp.zeros_like(own_cols)
+    other_cols[...] = jnp.zeros_like(other_cols)
+
+    def clear(i, carry):
+        at = pl.ds(pl.multiple_of(i * 256, 256), 256)
+        for w in range(WIN_DEV):
+            rows[w, at, :] = jnp.zeros((256, 128), jnp.float32)
+            for first, last in ((0, 32 * w), (32 * w + 32, 128)):
+                if last > first:
+                    own[w, pl.ds(first, last - first), at] = jnp.zeros((last - first, 256), jnp.bfloat16)
+                    other[w, pl.ds(first, last - first), at] = jnp.zeros((last - first, 256), jnp.bfloat16)
+        return carry
+
+    lax.fori_loop(0, TILE // 256, clear, 0)
+
     def chunk_of(q):
         return lax.bitwise_xor(my_slot // 8, q)
 
@@ -209,28 +222,42 @@
             cols[w, :, col_at] += fold_rows(a)
         return a[:, :128] + a[:, 128:]
 
-    if FAR_AFTER < 0:
-        lax.fori_loop(32, GROUPS, send, 0)
-    for q in range(4):
+    near, far = half * 8, 8 - half * 8
+
+    def against(row_block, col_chunk, w):
+        row_at = block(row_block)
+        rows[w, row_at, :] += pairs(w, row_at, block(2 * col_chunk), own, own_cols) + pairs(
+            w, row_at, block(2 * col_chunk + 1), own, own_cols
+        )
+
+    def with_chunk(q, r):
+        for i in range(2):
+            for w in range(WIN_DEV):
+                against(2 * chunk_of(r) + i, chunk_of(q), w)
+
+    def with_itself(q):
+        first, second = block(2 * chunk_of(q)), block(2 * chunk_of(q) + 1)
+        for w in range(WIN_DEV):
+            rows[w, first, :] += pairs(w, first, first, own, None) + pairs(w, first, second, own, own_cols)
+            rows[w, second, :] += pairs(w, second, second, own, None)
+
+    def next_chunk(q):
         receive(q)
-        if q == FAR_AFTER:
-            lax.fori_loop(32, GROUPS, send, 0)
         prepare_chunk(q)
+
+    next_chunk(0)
+    pl.semaphore_wait(far_ready, 1)
+    lax.fori_loop(32, GROUPS, send, 0, unroll=4)
+    settle_chunk(0)
+    with_itself(0)
+    pass_on(0)
+    for q in range(1, 4):
+        next_chunk(q)
         settle_chunk(q)
-        chunk = chunk_of(q)
-        first, second = block(2 * chunk), block(2 * chunk + 1)
-        for w in range(WIN_DEV):
-            one = pairs(w, first, first, own, None) + pairs(w, first, second, own, own_cols)
-            two = pairs(w, second, second, own, None)
-            for r in range(q):
-                for d in range(2):
-                    col_at = block(2 * chunk_of(r) + d)
-                    one = one + pairs(w, first, col_at, own, own_cols)
-                    two = two + pairs(w, second, col_at, own, own_cols)
-            rows[w, first, :] += one
-            rows[w, second, :] += two
+        for r in range(q):
+            with_chunk(q, r)
+        with_itself(q)
         pass_on(q)
-    near, far = half * 8, 8 - half * 8
 
     def with_near(q, w, i):
         row_at = block(2 * chunk_of(q) + i)
@@ -244,14 +271,12 @@
         for w in range(WIN_DEV):
             with_near(q, w, 0)
         pass_on(q)
-        receive(q + 1)
-        prepare_chunk(q + 1)
+        next_chunk(q + 1)
         for w in range(WIN_DEV):
             with_near(q, w, 1)
         return carry
 
-    receive(4)
-    prepare_chunk(4)
+    next_chunk(4)
     lax.fori_loop(4, 7, late, 0)
     settle_chunk(7)
     pass_on(7)
@@ -401,6 +426,7 @@
             pltpu.SemaphoreType.DMA((8, WIN_DEV)),
             pltpu.SemaphoreType.DMA((2,)),
             pltpu.SemaphoreType.DMA((2,)),
+            pltpu.SemaphoreType.REGULAR,
         ],
         compiler_params=pltpu.CompilerParams(collective_id=0, has_side_effects=True, vmem_limit_bytes=56 * 2**20),
         name="connect",

time: 51.8 us -> 50.5 us (0.975)
  Pallas kernels: 50.2 us -> 48.8 us
    pallas_call x1, Pallas kernels: 50.2 us -> 48.8 us  [shards(): pl.pallas_call(kernel, out_shape=jax.ShapeDtypeStruct((WIN_DEV, TILE), jn...]
where the time goes in v7:
time: 50.5 us; the launch traced here: 50.3 us
  Pallas kernels  48.8 us (97%)
  local copies, waits for them, and re-layouts  1.48 us (3%)
    pallas_call x1, Pallas kernels, shards(): pl.pallas_call(kernel, out_shape=jax.ShapeDtypeStruct((WIN_DEV, TILE), jn...  48.8 us
    unnamed x1, local copies, waits for them, and re-layouts  1.48 us

profile of v7, /device:TPU:1, one launch (start us, length us, event | category | flops | bytes accessed | tf_op | source)
XLA Modules:
  0.0 50.3 jit_solution(11198248254812574279)
XLA Ops:
  0.0 48.8 %connect.1 = f32[3,4096]{1,0:T(4,128)} custom-call(f32[480,128]{1,0:T(8,128)} %bitcast.2, f32[1,1600]{1,0:T(1,128)} %bitcast.3), custom_call_target="tpu_custom_call" | custom-call | tf_op jit(solution)/shard_map/connect/pallas_call | solution.py:399
  48.8 1.5 %copy.4 = f32[3,4096]{1,0:T(4,128)} copy(f32[3,4096]{1,0:T(4,128)} %connect.1) | data formatting | bytes 98304

commit v8 on v7

--- a/solution.py
+++ b/solution.py
@@ -245,14 +245,18 @@
         receive(q)
         prepare_chunk(q)
 
-    next_chunk(0)
+    receive(0)
     pl.semaphore_wait(far_ready, 1)
-    lax.fori_loop(32, GROUPS, send, 0, unroll=4)
+    lax.fori_loop(32, 48, send, 0, unroll=4)
+    prepare_chunk(0)
     settle_chunk(0)
     with_itself(0)
     pass_on(0)
     for q in range(1, 4):
-        next_chunk(q)
+        receive(q)
+        if q == 1:
+            lax.fori_loop(48, GROUPS, send, 0, unroll=4)
+        prepare_chunk(q)
         settle_chunk(q)
         for r in range(q):
             with_chunk(q, r)

time: 50.5 us -> 49.9 us (0.988)
    pallas_call x1, Pallas kernels: 48.8 us -> 48.3 us  [shards(): pl.pallas_call(kernel, out_shape=jax.ShapeDtypeStruct((WIN_DEV, TILE), jn...]
where the time goes in v8:
time: 49.9 us; the launch traced here: 49.8 us
  Pallas kernels  48.3 us (97%)
  local copies, waits for them, and re-layouts  1.48 us (3%)
    pallas_call x1, Pallas kernels, shards(): pl.pallas_call(kernel, out_shape=jax.ShapeDtypeStruct((WIN_DEV, TILE), jn...  48.3 us
    unnamed x1, local copies, waits for them, and re-layouts  1.48 us

profile of v8, /device:TPU:1, one launch (start us, length us, event | category | flops | bytes accessed | tf_op | source)
XLA Modules:
  0.0 49.8 jit_solution(11788806480556461422)
XLA Ops:
  0.0 48.3 %connect.1 = f32[3,4096]{1,0:T(4,128)} custom-call(f32[480,128]{1,0:T(8,128)} %bitcast.2, f32[1,1600]{1,0:T(1,128)} %bitcast.3), custom_call_target="tpu_custom_call" | custom-call | tf_op jit(solution)/shard_map/connect/pallas_call | solution.py:403
  48.3 1.5 %copy.4 = f32[3,4096]{1,0:T(4,128)} copy(f32[3,4096]{1,0:T(4,128)} %connect.1) | data formatting | bytes 98304

commit v9 on v8

--- a/solution.py
+++ b/solution.py
@@ -99,7 +99,7 @@
         pl.semaphore_signal(barrier, inc=1, device_id=(target, half), device_id_type=MESH)
         return carry
 
-    lax.fori_loop(0, 31, greet, 0)
+    lax.fori_loop(0, 31, greet, 0, unroll=4)
     pl.semaphore_signal(barrier, inc=1, device_id=(sibling, half), device_id_type=MESH)
     pl.semaphore_signal(barrier, inc=1, device_id=(me, 1 - half), device_id_type=MESH)
 
@@ -165,7 +165,7 @@
         remote(k).start()
         return carry
 
-    lax.fori_loop(1, 32, send, 0)
+    lax.fori_loop(1, 32, send, 0, unroll=4)
     _, _, kept = message(0)
     pltpu.make_async_copy(kept, own_raw.at[my_slot], own_sem.at[my_slot // 8]).start()
 

time: 49.9 us -> 49.9 us (level)
  no operation moved by 1% of the time
where the time goes in v9:
time: 49.9 us; the launch traced here: 49.6 us
  Pallas kernels  48.1 us (96%)
  local copies, waits for them, and re-layouts  1.48 us (3%)
    pallas_call x1, Pallas kernels, shards(): pl.pallas_call(kernel, out_shape=jax.ShapeDtypeStruct((WIN_DEV, TILE), jn...  48.1 us
    unnamed x1, local copies, waits for them, and re-layouts  1.48 us

profile of v9, /device:TPU:1, one launch (start us, length us, event | category | flops | bytes accessed | tf_op | source)
XLA Modules:
  0.0 49.6 jit_solution(2598003618295415470)
XLA Ops:
  0.0 48.1 %connect.1 = f32[3,4096]{1,0:T(4,128)} custom-call(f32[480,128]{1,0:T(8,128)} %bitcast.2, f32[1,1600]{1,0:T(1,128)} %bitcast.3), custom_call_target="tpu_custom_call" | custom-call | tf_op jit(solution)/shard_map/connect/pallas_call | solution.py:403
  48.2 1.5 %copy.4 = f32[3,4096]{1,0:T(4,128)} copy(f32[3,4096]{1,0:T(4,128)} %connect.1) | data formatting | bytes 98304
